TPU v7x, 32 devices: a whole 2x2x4 slice. The times are simulated.
32 devices in a mesh: dp: 2 (over x), ep: 16 (over z, y, core).
Axes of the slice: x: 2, y: 2, z: 4, core: 2. Of those that a mesh axis runs over, the one named last changes fastest.
Arguments:
- x_tokens: bfloat16 [4096, 1536], P(('dp', 'ep')), parts along dimension 0
- slot_expert: int32 [320], replicated
- w1_slots: bfloat16 [320, 1536, 512], P('ep')
- w3_slots: bfloat16 [320, 1536, 512], P('ep')
- w2_slots: bfloat16 [320, 512, 1536], P('ep')
- assign: int32 [4096, 6], P(('dp', 'ep')), parts along dimension 0
- w_router: bfloat16 [1536, 64], replicated
- w1_shared: bfloat16 [1536, 1024], replicated
- w3_shared: bfloat16 [1536, 1024], replicated
- w2_shared: bfloat16 [1024, 1536], replicated
Outputs:
- output: bfloat16 [4096, 1536], P(('dp', 'ep')), parts along dimension 0
There are 2 independent parts. A program takes and returns all parts, laid end to end along the dimension named above; an argument that names none is the same for every part.
All inputs are finite; a program needn't handle non-finite values.
Results may differ from a plain program's by a relative error of at most 0.001.
Values are sent between devices in bfloat16 or wider.
A program may use at most 1 GiB of HBM per device.

v0:
```python
import jax
import jax.numpy as jnp
from jax import lax
from jax.sharding import PartitionSpec as P

ROUTE_SCALE = 2.5


def gate_weights(x_tokens, assign, slot_expert, w_router):
    logits = jnp.dot(x_tokens, w_router, preferred_element_type=jnp.float32)
    gate_prob = jax.nn.sigmoid(logits)
    is_kept = assign >= 0
    chosen = jnp.take(slot_expert, jnp.maximum(assign, 0))
    picked = jnp.where(is_kept, jnp.take_along_axis(gate_prob, chosen, axis=1), 0.0)
    gate_total = jnp.sum(picked, axis=1, keepdims=True)
    return ROUTE_SCALE * picked / jnp.maximum(gate_total, 1e-30), is_kept


def shared_expert(x_tokens, w1_shared, w3_shared, w2_shared):
    h_gate = jnp.dot(x_tokens, w1_shared, preferred_element_type=jnp.float32)
    h_up = jnp.dot(x_tokens, w3_shared, preferred_element_type=jnp.float32)
    mid_act = (jax.nn.silu(h_gate) * h_up).astype(jnp.bfloat16)
    return jnp.dot(mid_act, w2_shared, preferred_element_type=jnp.float32)


def solution(mesh):
    group_size = mesh.shape['ep']

    def device_step(x_tokens, slot_expert, w1_slots, w3_slots, w2_slots, assign, w_router, w1_shared, w3_shared, w2_shared):
        tok_dev, dim_model = x_tokens.shape
        top_k = assign.shape[1]
        local_slots = w1_slots.shape[0]
        num_slots = local_slots * group_size
        cap_rows = max(4, (3 * tok_dev * top_k) // num_slots)
        route_weight, is_kept = gate_weights(x_tokens, assign, slot_expert, w_router)
        shared_out = shared_expert(x_tokens, w1_shared, w3_shared, w2_shared)
        flat_slot = jnp.where(is_kept, assign, num_slots).reshape(-1)
        onehot = (flat_slot[:, None] == jnp.arange(num_slots, dtype=jnp.int32)[None, :]).astype(jnp.int32)
        slot_rank = jnp.sum(jnp.cumsum(onehot, axis=0) * onehot, axis=1) - 1
        dummy_row = num_slots * cap_rows
        row_pos = jnp.where(flat_slot < num_slots, flat_slot * cap_rows + slot_rank, dummy_row)
        token_ids = jnp.arange(tok_dev * top_k, dtype=jnp.int32) // top_k
        row_token = jnp.full((dummy_row + 1,), tok_dev, jnp.int32).at[row_pos].set(token_ids)[:dummy_row]
        send_rows = jnp.take(x_tokens, row_token, axis=0, mode='fill', fill_value=0)
        recv_rows = lax.all_to_all(send_rows, 'ep', 0, 0, tiled=True)
        recv_rows = recv_rows.reshape(group_size, local_slots, cap_rows, dim_model)
        h_gate = jnp.einsum('jlcd,ldf->jlcf', recv_rows, w1_slots, preferred_element_type=jnp.float32)
        h_up = jnp.einsum('jlcd,ldf->jlcf', recv_rows, w3_slots, preferred_element_type=jnp.float32)
        mid_act = (jax.nn.silu(h_gate) * h_up).astype(jnp.bfloat16)
        expert_out = jnp.einsum('jlcf,lfd->jlcd', mid_act, w2_slots, preferred_element_type=jnp.float32).astype(jnp.bfloat16)
        back_rows = lax.all_to_all(expert_out.reshape(dummy_row, dim_model), 'ep', 0, 0, tiled=True)
        gathered = jnp.take(back_rows, jnp.minimum(row_pos, dummy_row - 1), axis=0).reshape(tok_dev, top_k, dim_model)
        routed = jnp.sum(route_weight[:, :, None] * gathered, axis=1)
        return (shared_out + routed).astype(jnp.bfloat16)

    token_spec = P(('dp', 'ep'), None)
    slot_spec = P('ep', None, None)
    return jax.shard_map(device_step, mesh=mesh, in_specs=(token_spec, P(), slot_spec, slot_spec, slot_spec, token_spec, P(), P(), P(), P()), out_specs=token_spec, check_vma=False)
```

profile of v0, /device:TPU:13, one launch (start us, length us, event | category | flops | bytes accessed | tf_op | source)
XLA Modules:
  0.0 471.4 jit_solution(9413843273159181512)
XLA Ops:
  8.9 1.5 broadcast_add_fusion
  13.0 1.5 compare_and_fusion
  14.5 1.4 lt.84
  15.9 1.6 mul.62
  18.8 4.1 scatter_custom_fusion
  24.8 8.9 %gather_fusion.1 = bf16[2240,1536]{1,0:T(8,128)(2,1)} fusion(bf16[128,1536]{1,0:T(8,128)(2,1)S(1)} %copy-done.2, s32[3072]{0:T(1024)} %pad_clamp_fusion), kind=kCustom, calls=%fused_computation.1 | custom fusion | bytes 13771520 | tf_op jit(solution)/shard_map/jit(_take)/gather | solution.py:44
  33.8 8.5 %gather.23 = bf16[16,140,1536]{2,1,0:T(8,128)(2,1)} reshape(bf16[2240,1536]{1,0:T(8,128)(2,1)} %gather_fusion.1) | data formatting | bytes 13762560 | tf_op jit(solution)/shard_map/jit(_take)/gather | solution.py:44
  42.4 3.6 broadcast_select_fusion
  46.0 160.5 %all_to_all.18 = bf16[16,140,1536]{2,1,0:T(8,128)(2,1)} all-to-all(bf16[16,140,1536]{2,1,0:T(8,128)(2,1)S(1)} %broadcast_select_fusion), channel_id=1, replica_groups=mesh['dp'=2,'ep'=16] {'ep'}, dimensions={0} | all-to-all | bytes 13762560 | tf_op jit(solution)/shard_map/all_to_all | solution.py:45
  206.5 9.7 %copy.22 = bf16[16,140,1536]{2,0,1:T(8,128)(2,1)} copy(bf16[16,140,1536]{2,1,0:T(8,128)(2,1)} %all_to_all.18) | data formatting | bytes 13762560 | tf_op jit(solution)/shard_map/all_to_all | solution.py:45
  216.2 18.9 %fusion.2 = f32[20,16,7,512]{3,1,2,0:T(8,128)} fusion(bf16[16,20,7,1536]{3,0,2,1:T(8,128)(2,1)} %bitcast.63, bf16[20,1536,512]{2,1,0:T(8,128)(2,1)} %param.13), kind=kOutput, calls=%fused_computation.7 | convolution fusion | flops 3523215360 | bytes 42926080 | tf_op jit(solution)/shard_map/jlcd,ldf->jlcf/dot_general | solution.py:48
  235.1 17.4 %fusion.9 = bf16[16,20,7,512]{3,0,2,1:T(8,128)(2,1)} fusion(f32[20,16,7,512]{3,1,2,0:T(8,128)} %fusion.2, bf16[16,20,7,1536]{3,0,2,1:T(8,128)(2,1)} %bitcast.64, bf16[20,1536,512]{2,1,0:T(8,128)(2,1)} %param.12), kind=kOutput, calls=%fused_computation.15 | convolution fusion | flops 3530096640 | bytes 45219840 | tf_op jit(solution)/shard_map/jlcd,ldf->jlcf/dot_general | solution.py:47
  252.5 16.1 %fusion.6 = bf16[20,16,7,1536]{3,1,2,0:T(8,128)(2,1)} fusion(bf16[16,20,7,512]{3,0,2,1:T(8,128)(2,1)} %fusion.9, bf16[20,512,1536]{2,1,0:T(8,128)(2,1)} %param.14), kind=kOutput, calls=%fused_computation.13 | convolution fusion | flops 3526656000 | bytes 40632320 | tf_op jit(solution)/shard_map/jlcf,lfd->jlcd/dot_general | solution.py:50
  268.6 9.7 %copy.23 = bf16[16,140,1536]{2,1,0:T(8,128)(2,1)} copy(bf16[16,140,1536]{2,0,1:T(8,128)(2,1)} %bitcast.65) | data formatting | bytes 13762560 | tf_op jit(solution)/shard_map/all_to_all | solution.py:51
  278.3 5.8 %all-to-all-start.1 = ((bf16[16,140,1536]{2,1,0:T(8,128)(2,1)}), bf16[16,140,1536]{2,1,0:T(8,128)(2,1)}, u32[]{:S(2)}, u32[]{:S(2)}) async-start(bf16[16,140,1536]{2,1,0:T(8,128)(2,1)} %copy.23), calls=%async_computation.1 | async-start | bytes 14155776 | tf_op jit(solution)/shard_map/all_to_all | solution.py:51
  284.3 5.0 %gather_fusion = s32[768]{0:T(1024)S(1)} fusion(s32[320]{0:T(512)S(1)} %copy-done.1, s32[1024]{0:T(1024)S(1)} %pad_clamp_fusion.2), kind=kCustom, calls=%fused_computation | custom fusion | bytes 9216 | tf_op jit(solution)/shard_map/jit(_take)/gather | solution.py:13
  291.0 5.1 %gather_fusion.3 = f32[768]{0:T(1024)S(1)} fusion(f32[128,64]{0,1:T(8,128)S(1)} %fusion.22, s32[768]{0:T(1024)S(1)} %reshape.176), kind=kCustom, calls=%fused_computation.3 | custom fusion | bytes 12288 | tf_op jit(solution)/shard_map/jit(take_along_axis)/gather | solution.py:14
  297.1 3.4 fusion.40
  300.5 138.1 %all-to-all-done.1 = bf16[16,140,1536]{2,1,0:T(8,128)(2,1)} async-done(((bf16[16,140,1536]{2,1,0:T(8,128)(2,1)}), bf16[16,140,1536]{2,1,0:T(8,128)(2,1)}, u32[]{:S(2)}, u32[]{:S(2)}) %all-to-all-start.1) | async-done | bytes 6881312 | tf_op jit(solution)/shard_map/all_to_all | solution.py:51
  438.6 8.6 %all_to_all.15 = bf16[2240,1536]{1,0:T(8,128)(2,1)} reshape(bf16[16,140,1536]{2,1,0:T(8,128)(2,1)} %all-to-all-done.1) | data formatting | bytes 13762560 | tf_op jit(solution)/shard_map/all_to_all | solution.py:51
  447.2 9.8 %gather_fusion.2 = bf16[768,1536]{1,0:T(8,128)(2,1)} fusion(bf16[2240,1536]{1,0:T(8,128)(2,1)} %all_to_all.15, s32[1024]{0:T(1024)S(1)} %pad_clamp_fusion.1), kind=kCustom, calls=%fused_computation.2 | custom fusion | bytes 4721664 | tf_op jit(solution)/shard_map/jit(_take)/gather | solution.py:52
  457.0 5.0 %gather.25 = bf16[128,6,1536]{2,1,0:T(8,128)(2,1)} reshape(bf16[768,1536]{1,0:T(8,128)(2,1)} %gather_fusion.2) | data formatting | bytes 4718592 | tf_op jit(solution)/shard_map/jit(_take)/gather | solution.py:52
  461.9 5.4 %multiply_reduce_fusion = f32[128,1536]{1,0:T(8,128)} fusion(bf16[128,6,1536]{2,1,0:T(8,128)(2,1)} %gather.25, f32[128,6]{1,0:T(8,128)} %multiply_divide_fusion, pred[128,6]{1,0:T(8,128)(4,1)S(1)} %copy-done.9), kind=kLoop, calls=%fused_computation.12 | loop fusion | flops 4521984 | bytes 3149568 | tf_op jit(solution)/shard_map/reduce_sum | solution.py:53
  467.3 4.1 fusion.15
  (57 shorter events, 17.5 us)
Async XLA Ops:
  0.0 467.3 %copy-start = (bf16[1024,1536]{1,0:T(8,128)(2,1)S(1)}, bf16[1024,1536]{1,0:T(8,128)(2,1)}, u32[]{:S(2)}) copy-start(bf16[1024,1536]{1,0:T(8,128)(2,1)} %param.19) | copy-start | bytes 9437188
  0.9 3.0 copy-start.5
  2.5 1.5 copy-start.7
  4.7 20.2 %copy-start.2 = (bf16[128,1536]{1,0:T(8,128)(2,1)S(1)}, bf16[128,1536]{1,0:T(8,128)(2,1)}, u32[]{:S(2)}) copy-start(bf16[128,1536]{1,0:T(8,128)(2,1)} %param.10) | copy-start | bytes 1179652
  5.8 1.2 copy-start.4
  8.9 1.8 copy-start.11
  33.8 8.5 %copy-start.10 = (s32[2240]{0:T(1024)S(1)}, s32[2240]{0:T(1024)}, u32[]{:S(2)}) copy-start(s32[2240]{0:T(1024)} %get-tuple-element.14) | copy-start | bytes 26884
  278.3 5.8 %copy-start.8 = (s32[128,6]{1,0:T(8,128)S(1)}, s32[128,6]{1,0:T(8,128)}, u32[]{:S(2)}) copy-start(s32[128,6]{1,0:T(8,128)} %get-tuple-element.13) | copy-start | bytes 9220
  278.3 5.9 %copy-start.1 = (s32[320]{0:T(512)S(1)}, s32[320]{0:T(512)}, u32[]{:S(2)}) copy-start(s32[320]{0:T(512)} %param.11) | copy-start | bytes 3844
  278.3 160.3 %all-to-all-start.1 = ((bf16[16,140,1536]{2,1,0:T(8,128)(2,1)}), bf16[16,140,1536]{2,1,0:T(8,128)(2,1)}, u32[]{:S(2)}, u32[]{:S(2)}) async-start(bf16[16,140,1536]{2,1,0:T(8,128)(2,1)} %copy.23), calls=%async_computation.1 | async-start | bytes 14155776 | tf_op jit(solution)/shard_map/all_to_all | solution.py:51
  284.3 5.2 %copy-start.6 = (s32[128,6]{1,0:T(8,128)S(1)}, s32[128,6]{1,0:T(8,128)}, u32[]{:S(2)}) copy-start(s32[128,6]{1,0:T(8,128)} %copy-done.5) | copy-start | bytes 9220
  290.9 5.3 %copy-start.12 = (s32[768]{0:T(1024)S(1)}, s32[768]{0:T(1024)}, u32[]{:S(2)}) copy-start(s32[768]{0:T(1024)} %get-tuple-element.5) | copy-start | bytes 9220
  457.0 5.0 %copy-start.9 = (pred[128,6]{1,0:T(8,128)(4,1)S(1)}, pred[128,6]{1,0:T(8,128)(4,1)}, u32[]{:S(2)}) copy-start(pred[128,6]{1,0:T(8,128)(4,1)} %get-tuple-element.7) | copy-start | bytes 2308
  457.0 10.4 %copy-start.3 = (bf16[128,1536]{1,0:T(8,128)(2,1)S(1)}, bf16[128,1536]{1,0:T(8,128)(2,1)}, u32[]{:S(2)}) copy-start(bf16[128,1536]{1,0:T(8,128)(2,1)} %param.10) | copy-start | bytes 1179652
where the time goes:
time: 473 us; the launch traced here: 471 us
  blocking collectives  161 us (34%)
  waiting for transfers between devices  138 us (29%)
  local copies, waits for them, and re-layouts  84.1 us (18%)
  matrix products  61.2 us (13%)
  other arithmetic  21.5 us (5%)
  starting transfers between devices  5.77 us (1%)
    all_to_all x1, blocking collectives, device_step(): recv_rows = lax.all_to_all(send_rows, 'ep', 0, 0, tiled=True)  161 us
    all_to_all x1, waiting for transfers between devices, device_step(): lax.all_to_all(expert_out.reshape(dummy_row, dim_model), 'ep', 0, 0, tile...  138 us
    dot_general x1, matrix products, device_step(): jnp.einsum('jlcd,ldf->jlcf', recv_rows, w3_slots, preferred_element_type=...  18.9 us
    all_to_all x2, local copies, waits for them, and re-layouts, device_step(): lax.all_to_all(expert_out.reshape(dummy_row, dim_model), 'ep', 0, 0, tile...  18.2 us
    gather x2, local copies, waits for them, and re-layouts, device_step(): send_rows = jnp.take(x_tokens, row_token, axis=0, mode='fill', fill_value=0)  17.5 us
    dot_general x1, matrix products, device_step(): jnp.einsum('jlcd,ldf->jlcf', recv_rows, w1_slots, preferred_element_type=...  17.4 us
    dot_general x1, matrix products, device_step(): jnp.einsum('jlcf,lfd->jlcd', mid_act, w2_slots, preferred_element_type=jn...  16.1 us
    gather x2, local copies, waits for them, and re-layouts, device_step(): jnp.take(back_rows, jnp.minimum(row_pos, dummy_row - 1), axis=0)  14.7 us
  transfers between devices with their start and end apart: 1, of which 1 were waited for; matrix products, arithmetic and copies ran while one was open for 3% of the time, Pallas kernels for 0%

commit v1 on v0

v1 whole, which is shorter than its diff:
```python
import functools

import jax
import jax.numpy as jnp
from jax import lax
from jax.experimental import pallas as pl
from jax.experimental.pallas import tpu as pltpu
from jax.sharding import PartitionSpec as P

ROUTE_SCALE = 2.5
MESH = pl.DeviceIdType.MESH
NUM_EXPERTS = 64
EXT = 64
UNIT = 128
NBUF = 6
F32, BF16, I32 = jnp.float32, jnp.bfloat16, jnp.int32


def dims():
    me = lax.axis_index("ep")
    c, y, z, h = me % 2, (me // 2) % 2, (me // 4) % 2, me // 8
    sib = me + 1 - 2 * c
    yn = me + 2 - 4 * y
    zn = me + 4 - 8 * z
    mir = me + 8 - 16 * h
    first = yn + c * (zn - yn)
    second = zn + c * (yn - zn)
    diag = yn + zn - me
    return me, c, h, sib, yn, zn, mir, first, second, diag


def barrier(peers):
    sem = pltpu.get_barrier_semaphore()
    for peer in peers:
        pl.semaphore_signal(sem, inc=1, device_id=peer, device_id_type=MESH)
    pl.semaphore_wait(sem, len(peers))


def dot(a, b, ca=1, cb=0):
    return lax.dot_general(a, b, (((ca,), (cb,)), ((), ())), preferred_element_type=F32)


def split3(v):
    hi = v.astype(BF16)
    rest = v - hi.astype(F32)
    mid = rest.astype(BF16)
    lo = (rest - mid.astype(F32)).astype(BF16)
    return hi, mid, lo


def gather_kernel(x_ref, at_ref, se_ref, wr_ref, rnd_ref, w1_hbm, w3_hbm, w2_hbm,
                  xm_out, xe_out, wm_out, we_out, own_out, gw_out, z_out, nr_out,
                  xs, xes, wms, wes, xcr, wcr, xsnd, wsnd, cand_s, own_s, flag_s, frecv,
                  w1s, w3s, w2s, ssem, rsem, lsem):
    me, c, h, sib, yn, zn, mir, first, second, diag = dims()
    dp = lax.axis_index("dp")
    qm, qf, qs, qg = me % 8, first % 8, second % 8, diag % 8
    loads = [pltpu.make_async_copy(a, b, lsem.at[i]) for i, (a, b) in
             enumerate(((w1_hbm, w1s), (w3_hbm, w3s), (w2_hbm, w2s)))]
    for cp in loads:
        cp.start()
    barrier([{"ep": sib}, {"ep": yn}, {"ep": zn}, {"ep": mir}, {"dp": 1 - dp}])

    def rcopy(src, dst, i, dev):
        return pltpu.make_async_remote_copy(src_ref=src, dst_ref=dst, send_sem=ssem.at[i], recv_sem=rsem.at[i],
                                            device_id=dev, device_id_type=MESH)

    def spread(own, buf, base):
        ep = lambda d: {"ep": d}
        return [rcopy(own, buf.at[qm], base, ep(first)), rcopy(own, buf.at[qm], base + 1, ep(second)),
                rcopy(own, buf.at[qm], base + 2, ep(sib)), rcopy(buf.at[qf], buf.at[qf], base + 3, ep(second)),
                rcopy(buf.at[qf], buf.at[qf], base + 4, ep(sib)), rcopy(buf.at[qs], buf.at[qs], base + 5, ep(sib)),
                rcopy(buf.at[qg], buf.at[qg], base + 6, ep(sib))]

    ax = spread(x_ref, xs, 0)
    for i in range(3):
        ax[i].start()

    n_slots = se_ref.shape[1]
    n_tok = x_ref.shape[0]
    rnd = rnd_ref[0:1, 0:1]
    first_round = jnp.where(rnd == 0.0, 1.0, 0.0)
    logits = lax.dot_general(wr_ref[...], x_ref[...], (((0,), (1,)), ((), ())), preferred_element_type=F32)
    gate = jax.nn.sigmoid(logits)
    expert_of = se_ref[...]
    eye = (lax.broadcasted_iota(I32, (NUM_EXPERTS, n_slots), 0) == expert_of).astype(F32)
    eye_bf = eye.astype(BF16)
    lane_slot = lax.broadcasted_iota(I32, (1, n_slots), 1)
    per_half = n_slots // 2
    here = jnp.where((lane_slot >= h * per_half) & (lane_slot < (h + 1) * per_half), 1.0, 0.0)
    avail = jnp.where(jnp.sum(eye * here, axis=1, keepdims=True) > 0.0, 1.0, 0.0)
    row_slot = lax.broadcasted_iota(I32, (n_slots, n_tok), 0)
    picks = []
    for k in range(6):
        hot = (row_slot == at_ref[k:k + 1, :]).astype(F32).astype(BF16)
        picks.append(dot(eye_bf, hot))
    chosen = functools.reduce(lambda a, b: a + b, picks)
    picked = gate * chosen
    total = jnp.sum(picked, axis=0, keepdims=True)
    weight = ROUTE_SCALE * picked / jnp.maximum(total, 1e-30)
    xs[qm] = x_ref[...]
    wm_own = weight * (avail * first_round)
    wsnd[0] = wm_own
    wms[qm] = wm_own
    aw = spread(wsnd.at[0], wms, 7)
    for i in range(3):
        aw[i].start()

    miss = [jnp.sum(p * (1.0 - avail), axis=0, keepdims=True) for p in picks]
    miss_all = jnp.concatenate(miss + [jnp.zeros((2, n_tok), F32)], axis=0)
    upper = (lax.broadcasted_iota(I32, (n_tok, n_tok), 0) < lax.broadcasted_iota(I32, (n_tok, n_tok), 1))
    before = dot(miss_all.astype(BF16), upper.astype(F32).astype(BF16))
    offset = -EXT * rnd
    count = jnp.zeros((1, 1), F32)
    row_ext = lax.broadcasted_iota(I32, (EXT, n_tok), 0).astype(F32)
    take = jnp.zeros((EXT, n_tok), F32)
    expert_hot = jnp.zeros((NUM_EXPERTS, EXT), F32)
    home = jnp.zeros((EXT, n_tok), F32)
    for k in range(6):
        sel = jnp.where((row_ext == before[k:k + 1, :] + offset) & (miss[k] > 0.0), 1.0, 0.0)
        take += sel
        expert_hot += dot(picks[k].astype(BF16), sel.astype(BF16), 1, 1)
        home += sel * jnp.sum(picks[k] * weight, axis=0, keepdims=True)
        mk = jnp.sum(miss[k], axis=1, keepdims=True)
        offset += mk
        count += mk
    gw_out[...] = home
    xsnd[...] = dot(take.astype(BF16), x_ref[...]).astype(BF16)
    wsnd[1] = jnp.concatenate([expert_hot, jnp.zeros((NUM_EXPERTS, 128 - EXT), F32)], axis=1)
    cross = [rcopy(xsnd, xcr, 28, {"ep": mir}), rcopy(wsnd.at[1], wcr, 29, {"ep": mir})]
    for cp in cross:
        cp.start()
    flag_s[0] = jnp.broadcast_to(jnp.floor((count + (EXT - 1)) * (1.0 / EXT)), (8, 128))
    steps = [rcopy(flag_s.at[i], frecv.at[i], 30 + i, d) for i, d in
             enumerate(({"dp": 1 - dp}, {"ep": sib}, {"ep": mir}, {"ep": zn}, {"ep": yn}))]
    steps[0].start()

    slot_row = lax.broadcasted_iota(I32, (n_slots, 128), 0)
    lane_dev = lax.broadcasted_iota(I32, (n_slots, 128), 1)
    lo = (lane_dev + 8 * h) * (n_slots // 16)
    block = ((slot_row >= lo) & (slot_row < lo + n_slots // 16) & (lane_dev < 8)).astype(F32).astype(BF16)
    cand = jnp.where(dot(eye_bf, block) > 0.0, 1.0, 0.0)
    n_cand = jnp.sum(cand, axis=1, keepdims=True)
    cand_s[...] = cand
    load0 = jnp.sum(cand * jnp.where(n_cand == 1.0, 1.0, 0.0), axis=0, keepdims=True)
    lane = lax.broadcasted_iota(I32, (1, 128), 1).astype(F32)

    def pick(e, load):
        row = cand_s[pl.ds(e, 1), :]
        key = jnp.where(row > 0.0, load * 256.0 + lane, 1e9)
        best = jnp.min(key, axis=1, keepdims=True)
        sel = jnp.where((key == best) & (row > 0.0), 1.0, 0.0)
        own_s[pl.ds(e, 1), :] = sel
        several = jnp.where(jnp.sum(row, axis=1, keepdims=True) > 1.0, 1.0, 0.0)
        return load + sel * several

    lax.fori_loop(0, NUM_EXPERTS, pick, load0)
    mine = jnp.where(lax.broadcasted_iota(I32, (8, 128), 1) == qm, 1.0, 0.0)
    own = dot(mine.astype(BF16), own_s[...].astype(BF16), 1, 1)
    own_out[...] = jnp.concatenate([own, jnp.zeros((8, 128 - NUM_EXPERTS), F32)], axis=1).astype(I32)

    for i in range(4):
        steps[i].wait()
        flag_s[i + 1] = jnp.maximum(flag_s[i], frecv[i])
        steps[i + 1].start()

    for a in (ax, aw):
        a[0].wait_recv()
        a[3].start()
        a[4].start()
    for a in (ax, aw):
        a[1].wait_recv()
        a[5].start()
    for cp in cross:
        cp.wait()
    xes[qm] = xcr[...]
    wes[qm] = wcr[...]
    ex = spread(xcr, xes, 14)
    ew = spread(wcr, wes, 21)
    for a in (ex, ew):
        for i in range(3):
            a[i].start()
    steps[4].wait()
    nr_out[...] = jnp.maximum(flag_s[4], frecv[4])

    for cp in loads:
        cp.wait()
    hg = dot(x_ref[...], w1s[...])
    hu = dot(x_ref[...], w3s[...])
    act = (jax.nn.silu(hg) * hu).astype(BF16)
    z_out[...] = dot(act, w2s[...]) * first_round

    for a in (ax, aw):
        a[3].wait_recv()
        a[6].start()
    for a in (ex, ew):
        a[0].wait_recv()
        a[3].start()
        a[4].start()
    for a in (ex, ew):
        a[1].wait_recv()
        a[5].start()
    for a in (ax, aw):
        for i in (2, 4, 5, 6):
            a[i].wait_recv()
    outs = [pltpu.make_async_copy(xs, xm_out, lsem.at[3]), pltpu.make_async_copy(wms, wm_out, lsem.at[4])]
    for cp in outs:
        cp.start()
    for a in (ex, ew):
        a[3].wait_recv()
        a[6].start()
    for a in (ex, ew):
        for i in (2, 4, 5, 6):
            a[i].wait_recv()
    outs += [pltpu.make_async_copy(xes, xe_out, lsem.at[5]), pltpu.make_async_copy(wes, we_out, lsem.at[6])]
    for cp in outs[2:]:
        cp.start()
    for a in (ax, aw, ex, ew):
        for cp in a:
            cp.wait_send()
    for cp in outs:
        cp.wait()


def expert_kernel(own_ref, se_ref, xm_hbm, xe_hbm, wm_ref, we_ref, w1_hbm, w3_hbm, w2_hbm, pm_out, pe_out,
                  xv, wrow, rank, pv, gt, ocat, b1, b3, b2, slots, experts, seen, wsem, xsem):
    me = lax.axis_index("ep")
    n_local = w1_hbm.shape[0]
    n_main, n_ext = 8 * 128, 8 * EXT
    n_tok = n_main + n_ext
    xl = [pltpu.make_async_copy(xm_hbm, xv.at[pl.ds(0, n_main)], xsem.at[0]),
          pltpu.make_async_copy(xe_hbm, xv.at[pl.ds(n_main, n_ext)], xsem.at[1])]
    for cp in xl:
        cp.start()

    def clear(e, carry):
        seen[e] = 0
        return carry

    lax.fori_loop(0, NUM_EXPERTS, clear, 0)

    def listing(s, n):
        e = se_ref[me * n_local + s]
        use = (own_ref[0, e] == 1) & (seen[e] == 0)

        @pl.when(use)
        def _():
            slots[n] = s
            experts[n] = e
            seen[e] = 1
        return jnp.where(use, n + 1, n)

    n_act = lax.fori_loop(0, n_local, listing, 0)

    def fetch(i):
        s, b = slots[i], lax.rem(i, NBUF)
        return [pltpu.make_async_copy(w1_hbm.at[s], b1.at[b], wsem.at[0, b]),
                pltpu.make_async_copy(w3_hbm.at[s], b3.at[b], wsem.at[1, b]),
                pltpu.make_async_copy(w2_hbm.at[s], b2.at[b], wsem.at[2, b])]

    def start(i):
        @pl.when(i < n_act)
        def _():
            for cp in fetch(i):
                cp.start()

    for i in range(NBUF):
        start(i)

    upper = (lax.broadcasted_iota(I32, (128, 128), 0) < lax.broadcasted_iota(I32, (128, 128), 1))
    upper = upper.astype(F32).astype(BF16)
    run = jnp.zeros((NUM_EXPERTS, 1), F32)
    for j in range(n_tok // 128):
        if j < 8:
            w = wm_ref[j]
        else:
            w = jnp.concatenate([we_ref[2 * (j - 8)][:, :EXT], we_ref[2 * (j - 8) + 1][:, :EXT]], axis=1)
        mask = jnp.where(w != 0.0, 1.0, 0.0)
        pos = dot(mask.astype(BF16), upper) + run
        run += jnp.sum(mask, axis=1, keepdims=True)
        rank[:, j * 128:(j + 1) * 128] = jnp.where(mask > 0.0, pos, -1.0)
        wrow[:, j * 128:(j + 1) * 128] = w
    pv[...] = jnp.zeros_like(pv)
    for cp in xl:
        cp.wait()

    def one(i, carry):
        for cp in fetch(i):
            cp.wait()
        e, b = experts[i], lax.rem(i, NBUF)
        pos = rank[pl.ds(e, 1), :]
        units = (jnp.max(pos).astype(I32) + UNIT) // UNIT

        def unit(u, carry):
            rows = lax.broadcasted_iota(I32, (UNIT, n_tok), 0) + u * UNIT
            hit = rows.astype(F32) == rank[pl.ds(e, 1), :]
            g = jnp.where(hit, 1.0, 0.0)
            wcol = jnp.sum(jnp.where(hit, wrow[pl.ds(e, 1), :], 0.0), axis=1, keepdims=True)
            xg = dot(g.astype(BF16), xv[...]).astype(BF16)
            act = (jax.nn.silu(dot(xg, b1[b])) * dot(xg, b3[b])).astype(BF16)
            o = dot(act, b2[b]).astype(BF16)
            for j, part in enumerate(split3(wcol * o.astype(F32))):
                ocat[j * UNIT:(j + 1) * UNIT, :] = part
            gt[...] = jnp.transpose(g).astype(BF16)

            def rows_of(m, carry):
                rs = pl.ds(pl.multiple_of(m * 256, 256), 256)
                left = gt[rs, :]
                pv[rs, :] += dot(jnp.concatenate([left, left, left], axis=1), ocat[...])
                return carry
            return lax.fori_loop(0, n_tok // 256, rows_of, carry)

        lax.fori_loop(0, units, unit, 0)
        start(i + NBUF)
        return carry

    lax.fori_loop(0, n_act, one, 0)
    outs = [pltpu.make_async_copy(pv.at[pl.ds(0, n_main)], pm_out, xsem.at[0]),
            pltpu.make_async_copy(pv.at[pl.ds(n_main, n_ext)], pe_out, xsem.at[1])]
    for cp in outs:
        cp.start()
    for cp in outs:
        cp.wait()


def scatter_kernel(pm_hbm, pe_hbm, acc_ref, z_ref, gw_ref, out_ref,
                   mo, md, mrg, mrf, mrs, mfin, eo, ed, erg, erf, ers, efin, esnd, ecr, ssem, rsem, lsem):
    me, c, h, sib, yn, zn, mir, first, second, diag = dims()
    cols = mo.shape[-1]
    mine = pl.ds(pl.multiple_of(c * cols, 128), cols)
    theirs = pl.ds(pl.multiple_of((1 - c) * cols, 128), cols)
    chips = [(d % 8) // 2 for d in (diag, first, second, me)]
    local, peer = [], []
    for base, (src, own, got) in ((0, (pe_hbm, eo, ed)), (4, (pm_hbm, mo, md))):
        for i, chip in enumerate(chips):
            rows = pl.ds(2 * chip, 2)
            sib_rows = pl.ds(2 * chips[(0, 2, 1, 3)[i]], 2)
            local.append(pltpu.make_async_copy(src.at[rows, :, mine], own.at[i], lsem.at[base + i]))
            peer.append(pltpu.make_async_remote_copy(
                src_ref=src.at[sib_rows, :, theirs], dst_ref=got.at[i], send_sem=ssem.at[base + i],
                recv_sem=rsem.at[base + i], device_id={"ep": sib}, device_id_type=MESH))
    for cp in local:
        cp.start()
    barrier([{"ep": sib}, {"ep": yn}, {"ep": zn}, {"ep": mir}])
    for cp in peer:
        cp.start()

    def rcopy(src, dst, i, dev):
        return pltpu.make_async_remote_copy(src_ref=src, dst_ref=dst, send_sem=ssem.at[i], recv_sem=rsem.at[i],
                                            device_id={"ep": dev}, device_id_type=MESH)

    def sends(own, rg, rf, rs, fin, base):
        return [rcopy(own.at[0], rg, base, first), rcopy(own.at[1], rf, base + 1, first),
                rcopy(own.at[2], rs, base + 2, second), rcopy(own.at[3, 1 - c], fin, base + 3, sib)]

    se = sends(eo, erg, erf, ers, efin, 8)
    sm = sends(mo, mrg, mrf, mrs, mfin, 12)
    back = rcopy(esnd, ecr, 16, mir)

    def joined(own, got, i, base):
        local[base + i].wait()
        peer[base + i].wait_recv()
        own[i] = own[i] + got[i]

    joined(eo, ed, 0, 0)
    se[0].start()
    joined(mo, md, 0, 4)
    sm[0].start()
    joined(eo, ed, 1, 0)
    se[1].start()
    joined(mo, md, 1, 4)
    sm[1].start()
    joined(eo, ed, 2, 0)
    joined(eo, ed, 3, 0)
    joined(mo, md, 2, 4)
    joined(mo, md, 3, 4)
    se[0].wait_recv()
    eo[2] = eo[2] + erg[...]
    se[2].start()
    sm[0].wait_recv()
    mo[2] = mo[2] + mrg[...]
    sm[2].start()
    se[1].wait_recv()
    se[2].wait_recv()
    eo[3] = eo[3] + erf[...] + ers[...]
    se[3].start()
    se[3].wait_recv()
    esnd[:, mine] = eo[3, c].astype(BF16)
    esnd[:, theirs] = efin[...].astype(BF16)
    back.start()
    sm[1].wait_recv()
    mo[3] = mo[3] + mrf[...]
    back.wait_recv()
    out_ref[...] = acc_ref[...] + z_ref[...]
    for part in split3(gw_ref[...]):
        out_ref[...] += dot(part, ecr[...], 0, 0)
    sm[2].wait_recv()
    mo[3] = mo[3] + mrs[...]
    sm[3].start()
    out_ref[:, mine] += mo[3, c]
    sm[3].wait_recv()
    out_ref[:, theirs] += mfin[...]
    for cp in peer + se + sm + [back]:
        cp.wait_send()


def solution(mesh):
    any_space = pl.BlockSpec(memory_space=pl.ANY)
    vmem = pl.BlockSpec(memory_space=pltpu.VMEM)
    smem = pl.BlockSpec(memory_space=pltpu.SMEM)
    sds = jax.ShapeDtypeStruct

    def gather(x, at, se, wr, rnd, w1, w3, w2):
        d, ff = w1.shape
        return pl.pallas_call(
            gather_kernel,
            out_shape=(sds((8, 128, d), BF16), sds((8, EXT, d), BF16), sds((8, NUM_EXPERTS, 128), F32),
                       sds((8, NUM_EXPERTS, 128), F32), sds((8, 128), I32), sds((EXT, 128), F32),
                       sds((128, d), F32), sds((8, 128), F32)),
            in_specs=[vmem] * 5 + [any_space] * 3,
            out_specs=(any_space,) * 4 + (vmem,) * 4,
            scratch_shapes=[
                pltpu.VMEM((8, 128, d), BF16), pltpu.VMEM((8, EXT, d), BF16),
                pltpu.VMEM((8, NUM_EXPERTS, 128), F32), pltpu.VMEM((8, NUM_EXPERTS, 128), F32),
                pltpu.VMEM((EXT, d), BF16), pltpu.VMEM((NUM_EXPERTS, 128), F32),
                pltpu.VMEM((EXT, d), BF16), pltpu.VMEM((2, NUM_EXPERTS, 128), F32),
                pltpu.VMEM((NUM_EXPERTS, 128), F32), pltpu.VMEM((NUM_EXPERTS, 128), F32),
                pltpu.VMEM((5, 8, 128), F32), pltpu.VMEM((5, 8, 128), F32),
                pltpu.VMEM((d, ff), BF16), pltpu.VMEM((d, ff), BF16), pltpu.VMEM((ff, d), BF16),
                pltpu.SemaphoreType.DMA((35,)), pltpu.SemaphoreType.DMA((35,)), pltpu.SemaphoreType.DMA((7,)),
            ],
            compiler_params=pltpu.CompilerParams(collective_id=0, has_side_effects=True),
            name="gather_rows",
        )(x, at, se, wr, rnd, w1, w3, w2)

    def experts(own, se, xm, xe, wm, we, w1, w3, w2):
        _, d, ff = w1.shape
        n_tok = 8 * (128 + EXT)
        return pl.pallas_call(
            expert_kernel,
            out_shape=(sds((8 * 128, d), F32), sds((8 * EXT, d), F32)),
            in_specs=[smem, smem, any_space, any_space, vmem, vmem] + [any_space] * 3,
            out_specs=(any_space, any_space),
            scratch_shapes=[
                pltpu.VMEM((n_tok, d), BF16), pltpu.VMEM((NUM_EXPERTS, n_tok), F32), pltpu.VMEM((NUM_EXPERTS, n_tok), F32),
                pltpu.VMEM((n_tok, d), F32), pltpu.VMEM((n_tok, UNIT), BF16), pltpu.VMEM((3 * UNIT, d), BF16),
                pltpu.VMEM((NBUF, d, ff), BF16), pltpu.VMEM((NBUF, d, ff), BF16), pltpu.VMEM((NBUF, ff, d), BF16),
                pltpu.SMEM((32,), I32), pltpu.SMEM((32,), I32), pltpu.SMEM((NUM_EXPERTS,), I32),
                pltpu.SemaphoreType.DMA((3, NBUF)), pltpu.SemaphoreType.DMA((2,)),
            ],
            name="expert_rows",
        )(own, se, xm, xe, wm, we, w1, w3, w2)

    def scatter(pm, pe, acc, z, gw):
        d = acc.shape[1]
        half = d // 2
        big, small = (2, 128, half), (2, EXT, half)
        return pl.pallas_call(
            scatter_kernel,
            out_shape=sds((128, d), F32),
            in_specs=[any_space, any_space, vmem, vmem, vmem],
            out_specs=vmem,
            scratch_shapes=[
                pltpu.VMEM((4,) + big, F32), pltpu.VMEM((4,) + big, F32),
                pltpu.VMEM(big, F32), pltpu.VMEM(big, F32), pltpu.VMEM(big, F32), pltpu.VMEM((128, half), F32),
                pltpu.VMEM((4,) + small, F32), pltpu.VMEM((4,) + small, F32),
                pltpu.VMEM(small, F32), pltpu.VMEM(small, F32), pltpu.VMEM(small, F32), pltpu.VMEM((EXT, half), F32),
                pltpu.VMEM((EXT, d), BF16), pltpu.VMEM((EXT, d), BF16),
                pltpu.SemaphoreType.DMA((17,)), pltpu.SemaphoreType.DMA((17,)), pltpu.SemaphoreType.DMA((8,)),
            ],
            compiler_params=pltpu.CompilerParams(collective_id=1, has_side_effects=True),
            name="scatter_sums",
        )(pm, pe, acc, z, gw)

    def device_step(x, slot_expert, w1, w3, w2, assign, wr, w1s, w3s, w2s):
        d = x.shape[1]
        at = jnp.concatenate([assign.T, jnp.full((2, assign.shape[0]), -1, I32)], axis=0)
        se = slot_expert.reshape(1, -1)

        def body(carry):
            r, _, acc = carry
            rnd = jnp.full((8, 128), r.astype(F32))
            xm, xe, wm, we, own, gw, z, nr = gather(x, at, se, wr, rnd, w1s, w3s, w2s)
            pm, pe = experts(own, slot_expert, xm.reshape(-1, d), xe.reshape(-1, d), wm, we, w1, w3, w2)
            acc = scatter(pm.reshape(8, 128, d), pe.reshape(8, EXT, d), acc, z, gw)
            return r + 1, nr[0, 0].astype(I32), acc

        carry = (jnp.int32(0), jnp.int32(1), jnp.zeros(x.shape, F32))
        out = lax.while_loop(lambda s: s[0] < s[1], body, carry)[2]
        return out.astype(BF16)

    tok = P(("dp", "ep"), None)
    slot = P("ep", None, None)
    return jax.shard_map(device_step, mesh=mesh,
                         in_specs=(tok, P(), slot, slot, slot, tok, P(), P(), P(), P()),
                         out_specs=tok, check_vma=False)
```

time: 473 us -> 157 us (0.33)
  the two profiles are of different devices: /device:TPU:13 before, /device:TPU:0 now
where the time goes in v1:
time: 157 us
  Pallas kernels  150 us (96%)
  local copies, waits for them, and re-layouts  5.28 us (3%)
    pallas_call x1, Pallas kernels, scatter(): pl.pallas_call(scatter_kernel, out_shape=sds((128, d), F32), in_specs=[an...  58.8 us
    pallas_call x1, Pallas kernels, experts(): pl.pallas_call(expert_kernel, out_shape=(sds((8 * 128, d), F32), sds((8 *...  50.9 us
    pallas_call x1, Pallas kernels, gather(): pl.pallas_call(gather_kernel, out_shape=(sds((8, 128, d), BF16), sds((8,...  40.4 us

profile of v1, /device:TPU:0, one launch (start us, length us, event | category | flops | bytes accessed | tf_op | source)
XLA Modules:
  0.0 156.9 jit_solution(14495584181716388629)
XLA Ops:
  0.0 0.7 reshape.16
  0.7 0.7 concatenate.3
  1.4 1.1 copy.11
  2.5 0.1 broadcast_in_dim.7
  2.6 153.5 %while.12 = (s32[]{:T(128)}, s32[]{:T(128)}, f32[128,1536]{1,0:T(8,128)S(1)}, bf16[128,1536]{1,0:T(8,128)(2,1)}, s32[8,128]{1,0:T(8,128)S(1)}, /*index=5*/s32[1,...) while((s32[]{:T(128)}, s32[]{:T(128)}, ...), condition=%wide.region_1.0_spmd, body=%wide.region_0.0_spmd.sunk | while | flops 4 | bytes 1582277 | solution.py:489
  2.6 0.9 copy.24.acc_ref
  3.5 0.6 broadcast_in_dim.9.rnd_ref
  4.1 0.0 copy-start
  4.1 40.4 %gather_rows.1 = (bf16[8,128,1536]{2,1,0:T(8,128)(2,1)}, bf16[8,64,1536]{2,1,0:T(8,128)(2,1)}, f32[8,64,128]{2,1,0:T(8,128)}, f32[8,64,128]{2,1,0:T(8,128)}, s32...) custom-call(bf16[128,1536]{1,0:T(8,128)(2,1)} %get-tuple-element.267.x_ref, ...), custom_call_target="tpu_custom_call" | custom-call | tf_op jit(solution)/shard_map/while/body/gather_rows/pallas_call | solution.py:415
  44.5 1.2 slice.4
  46.4 0.0 copy-done
  46.4 50.9 %expert_rows.1 = (f32[1024,1536]{1,0:T(8,128)}, f32[512,1536]{1,0:T(8,128)}) custom-call(s32[8,128]{1,0:T(8,128)} %get-tuple-element.225.own_ref, s32[320]{0:T(512)S(1)} %copy-done, bf16[1024,1536]{1,0:T(8,128)(2,1)} %bitcast.17, bf16[512,1536]{1,0:T(8,128)(2,1)} %bitcast.19, f32[8,64,128]{2,1,0:T(8,128)} %get-tuple-element.228.wm_ref, ...), custom_call_target="tpu_custom_call" | custom-call | tf_op jit(solution)/shard_map/while/body/expert_rows/pallas_call | solution.py:439
  97.3 58.8 %scatter_sums.1 = f32[128,1536]{1,0:T(8,128)S(1)} custom-call(f32[8,128,1536]{2,1,0:T(8,128)} %bitcast.16, f32[8,64,1536]{2,1,0:T(8,128)} %bitcast.18, f32[128,1536]{1,0:T(8,128)} %copy.24.acc_ref, f32[128,1536]{1,0:T(8,128)} %get-tuple-element.232.z_ref, f32[64,128]{1,0:T(8,128)} %get-tuple-element.233.gw_ref), custom_call_target="tpu_custom_call" | custom-call | tf_op jit(solution)/shard_map/while/body/scatter_sums/pallas_call | solution.py:458
  156.1 0.8 convert_element_type.12
Async XLA Ops:
  4.1 42.3 %copy-start = (s32[320]{0:T(512)S(1)}, s32[320]{0:T(512)}, u32[]{:S(2)}) copy-start(s32[320]{0:T(512)} %get-tuple-element.274.se_ref) | copy-start | bytes 3844 | tf_op jit(solution)/shard_map/while

commit v2 on v1

v2 whole, which is shorter than its diff:
```python
import functools

import jax
import jax.numpy as jnp
from jax import lax
from jax.experimental import pallas as pl
from jax.experimental.pallas import tpu as pltpu
from jax.sharding import PartitionSpec as P

ROUTE_SCALE = 2.5
MESH = pl.DeviceIdType.MESH
NUM_EXPERTS = 64
EXT = 64
UNIT = 128
PIECES = 2
NBUF = 6
MAXENT = 16
GROUP = 16
TILES = 160
TILE = 16
F32, BF16, I32 = jnp.float32, jnp.bfloat16, jnp.int32


def dims():
    me = lax.axis_index("ep")
    c, y, z, h = me % 2, (me // 2) % 2, (me // 4) % 2, me // 8
    sib = me + 1 - 2 * c
    yn = me + 2 - 4 * y
    zn = me + 4 - 8 * z
    mir = me + 8 - 16 * h
    first = yn + c * (zn - yn)
    second = zn + c * (yn - zn)
    diag = yn + zn - me
    return me, c, h, sib, yn, zn, mir, first, second, diag


def barrier(peers):
    sem = pltpu.get_barrier_semaphore()
    for peer in peers:
        pl.semaphore_signal(sem, inc=1, device_id=peer, device_id_type=MESH)
    pl.semaphore_wait(sem, len(peers))


def dot(a, b, ca=1, cb=0):
    return lax.dot_general(a, b, (((ca,), (cb,)), ((), ())), preferred_element_type=F32)


def split3(v):
    hi = v.astype(BF16)
    rest = v - hi.astype(F32)
    mid = rest.astype(BF16)
    lo = (rest - mid.astype(F32)).astype(BF16)
    return hi, mid, lo


def gather_kernel(x_ref, at_ref, se_ref, rnd_ref, wr_ref, w1_hbm, w3_hbm, w2_hbm,
                  xm_out, xe_out, wm_out, we_out, own_out, gw_out, z_out, nr_out,
                  xs, xes, wms, wes, xcr, ecr, xsnd, esnd, wsnd, cand_s, own_s, flag_s, frecv,
                  w1s, w3s, w2s, ssem, rsem, lsem):
    me, c, h, sib, yn, zn, mir, first, second, diag = dims()
    dp = lax.axis_index("dp")
    qm, qf, qs, qg = me % 8, first % 8, second % 8, diag % 8
    loads = [pltpu.make_async_copy(a, b, lsem.at[i]) for i, (a, b) in
             enumerate(((w1_hbm, w1s), (w3_hbm, w3s), (w2_hbm, w2s)))]
    for cp in loads:
        cp.start()
    barrier([{"ep": sib}, {"ep": yn}, {"ep": zn}, {"ep": mir}, {"dp": 1 - dp}])

    def rcopy(src, dst, i, dev):
        return pltpu.make_async_remote_copy(src_ref=src, dst_ref=dst, send_sem=ssem.at[i], recv_sem=rsem.at[i],
                                            device_id=dev, device_id_type=MESH)

    def spread(own, buf, base, one, two):
        ep = lambda d: {"ep": d}
        q1, q2 = one % 8, two % 8
        return [rcopy(own, buf.at[qm], base, ep(one)), rcopy(own, buf.at[qm], base + 1, ep(two)),
                rcopy(own, buf.at[qm], base + 2, ep(sib)), rcopy(buf.at[q1], buf.at[q1], base + 3, ep(two)),
                rcopy(buf.at[q1], buf.at[q1], base + 4, ep(sib)), rcopy(buf.at[q2], buf.at[q2], base + 5, ep(sib)),
                rcopy(buf.at[qg], buf.at[qg], base + 6, ep(sib))]

    parts = [pl.ds(i * (x_ref.shape[0] // PIECES), x_ref.shape[0] // PIECES) for i in range(PIECES)]
    ax = [spread(x_ref.at[r], xs.at[:, r], 45 + 7 * i, first, second) for i, r in enumerate(parts)]
    for i in range(2):
        ax[0][i].start()

    n_tok = x_ref.shape[0]
    n_slots = se_ref.shape[0]
    rnd = jnp.full((1, 1), rnd_ref[0], I32).astype(F32)
    first_round = jnp.where(rnd == 0.0, 1.0, 0.0)
    expert_of = se_ref[...].reshape(1, n_slots)
    eye = (lax.broadcasted_iota(I32, (NUM_EXPERTS, n_slots), 0) == expert_of).astype(F32)
    eye_bf = eye.astype(BF16)
    lane_slot = lax.broadcasted_iota(I32, (1, n_slots), 1)
    per_half = n_slots // 2
    here = jnp.where((lane_slot >= h * per_half) & (lane_slot < (h + 1) * per_half), 1.0, 0.0)
    avail = jnp.where(jnp.sum(eye * here, axis=1, keepdims=True) > 0.0, 1.0, 0.0)
    row_slot = lax.broadcasted_iota(I32, (n_slots, n_tok), 0)
    hot = jnp.concatenate([(row_slot == at_ref[k:k + 1, :]).astype(F32).astype(BF16) for k in range(6)], axis=1)
    picks_all = dot(eye_bf, hot)
    picks = [picks_all[:, k * n_tok:(k + 1) * n_tok] for k in range(6)]
    code = lax.broadcasted_iota(I32, (NUM_EXPERTS, n_tok), 0).astype(F32) + 1.0
    ids = [jnp.sum(p * code, axis=0, keepdims=True) for p in picks]
    miss = [jnp.sum(p * (1.0 - avail), axis=0, keepdims=True) for p in picks]
    none = jnp.zeros((2, n_tok), F32)
    id_all = jnp.concatenate(ids + [none], axis=0)
    miss_all = jnp.concatenate(miss + [none], axis=0)

    upper = (lax.broadcasted_iota(I32, (n_tok, n_tok), 0) < lax.broadcasted_iota(I32, (n_tok, n_tok), 1))
    before = dot(miss_all.astype(BF16), upper.astype(F32).astype(BF16))
    offset = -EXT * rnd
    count = jnp.zeros((1, 1), F32)
    row_ext = lax.broadcasted_iota(I32, (EXT, n_tok), 0).astype(F32)
    sels = []
    for k in range(6):
        sels.append(jnp.where((row_ext == before[k:k + 1, :] + offset) & (miss[k] > 0.0), 1.0, 0.0))
        mk = jnp.sum(miss[k], axis=1, keepdims=True)
        offset += mk
        count += mk
    take = functools.reduce(lambda a, b: a + b, sels)
    xsnd[...] = dot(take.astype(BF16), x_ref[...]).astype(BF16)
    piece = [pl.ds(i * (EXT // PIECES), EXT // PIECES) for i in range(PIECES)]
    cross = [rcopy(xsnd.at[r], xcr.at[r], 20 + i, {"ep": mir}) for i, r in enumerate(piece)]
    cross.append(rcopy(esnd, ecr, 19, {"ep": mir}))
    for cp in cross[:-1]:
        cp.start()
    codes = jnp.zeros((8, EXT), F32)
    for k in range(6):
        codes += dot(jnp.broadcast_to(ids[k], (8, n_tok)).astype(BF16), sels[k].astype(BF16), 1, 1)
    esnd[...] = jnp.concatenate([codes, jnp.zeros((8, 128 - EXT), F32)], axis=1)
    cross[-1].start()
    for a in ax[1:]:
        for i in range(2):
            a[i].start()
    for a in ax:
        a[2].start()

    gate = jax.nn.sigmoid(dot(wr_ref[...], x_ref[...], 1, 1))
    picked = gate * functools.reduce(lambda a, b: a + b, picks)
    total = jnp.sum(picked, axis=0, keepdims=True)
    weight = ROUTE_SCALE * picked / jnp.maximum(total, 1e-30)
    wk = [jnp.sum(p * weight, axis=0, keepdims=True) for p in picks]
    w_all = jnp.concatenate(wk + [none], axis=0) * (1.0 - miss_all) * first_round
    packed = jnp.concatenate([id_all, w_all], axis=0)
    wsnd[...] = packed
    wms[qm] = packed
    aw = spread(wsnd, wms, 7, first, second)
    for i in range(3):
        aw[i].start()
    gw_out[...] = functools.reduce(lambda a, b: a + b, [sel * w for sel, w in zip(sels, wk)])
    flag_s[0] = jnp.broadcast_to(jnp.floor((count + (EXT - 1)) * (1.0 / EXT)), (8, 128))
    steps = [rcopy(flag_s.at[i], frecv.at[i], 14 + i, d) for i, d in
             enumerate(({"dp": 1 - dp}, {"ep": sib}, {"ep": mir}, {"ep": zn}, {"ep": yn}))]
    steps[0].start()

    def vote(i):
        steps[i].wait()
        flag_s[i + 1] = jnp.maximum(flag_s[i], frecv[i])
        steps[i + 1].start()

    outs = []

    def put_out(src, dst, i):
        outs.append(pltpu.make_async_copy(src, dst, lsem.at[i]))
        outs[-1].start()

    put_out(x_ref, xm_out.at[qm], 3)

    slot_row = lax.broadcasted_iota(I32, (n_slots, 128), 0)
    lane_dev = lax.broadcasted_iota(I32, (n_slots, 128), 1)
    lo = (lane_dev + 8 * h) * (n_slots // 16)
    block = ((slot_row >= lo) & (slot_row < lo + n_slots // 16) & (lane_dev < 8)).astype(F32).astype(BF16)
    cand = jnp.where(dot(eye_bf, block) > 0.0, 1.0, 0.0)
    several = jnp.where(jnp.sum(cand, axis=1, keepdims=True) > 1.0, 1.0, 0.0)
    lane = lax.broadcasted_iota(I32, (1, 128), 1).astype(F32)
    block_key = jnp.where(cand > 0.0, jnp.broadcast_to(lane, cand.shape), 1e9)
    cand_s[0] = block_key
    there = jnp.where(jnp.sum(eye * (1.0 - here), axis=1, keepdims=True) > 0.0, 1.0, 2.0)
    cand_s[1] = jnp.broadcast_to(several * there, cand.shape)
    load0 = jnp.sum(cand * (1.0 - several) * there, axis=0, keepdims=True)

    def pick(e, load):
        key = cand_s[0, pl.ds(e, 1), :] + load * 256.0
        best = jnp.min(key, axis=1, keepdims=True)
        sel = jnp.where((key == best) & (key < 1e8), 1.0, 0.0)
        own_s[pl.ds(e, 1), :] = sel
        return load + sel * cand_s[1, pl.ds(e, 1), :]

    load1 = lax.fori_loop(0, NUM_EXPERTS // 2, pick, load0)
    vote(0)

    for a in ax + [aw]:
        a[0].wait_recv()
        a[3].start()
        a[4].start()
    for a in ax + [aw]:
        a[1].wait_recv()
        a[5].start()
    put_out(xs.at[qf], xm_out.at[qf], 4)
    put_out(xs.at[qs], xm_out.at[qs], 5)
    vote(1)
    lax.fori_loop(NUM_EXPERTS // 2, NUM_EXPERTS, pick, load1)
    mine = jnp.where(lax.broadcasted_iota(I32, (8, 128), 1) == qm, 1.0, 0.0)
    own = dot(mine.astype(BF16), own_s[...].astype(BF16), 1, 1)
    own_out[...] = jnp.concatenate([own, jnp.zeros((8, 128 - NUM_EXPERTS), F32)], axis=1).astype(I32)
    vote(2)

    ew = spread(ecr, wes, 24, zn, yn)
    ex = [spread(xcr.at[r], xes.at[:, r], 31 + 7 * i, zn, yn) for i, r in enumerate(piece)]
    for i, a in enumerate(ex):
        cross[i].wait_recv()
        for n in range(3):
            a[n].start()
    cross[-1].wait_recv()
    wes[qm] = ecr[...]
    for n in range(3):
        ew[n].start()
    put_out(xcr, xe_out.at[qm], 6)
    vote(3)

    for cp in loads:
        cp.wait()
    hg = dot(x_ref[...], w1s[...])
    hu = dot(x_ref[...], w3s[...])
    act = (jax.nn.silu(hg) * hu).astype(BF16)
    z_out[...] = dot(act, w2s[...]) * first_round

    for a in ex + [ew]:
        a[0].wait_recv()
        a[3].start()
        a[4].start()
    for a in ex + [ew]:
        a[1].wait_recv()
        a[5].start()
    put_out(xes.at[zn % 8], xe_out.at[zn % 8], 7)
    put_out(xes.at[yn % 8], xe_out.at[yn % 8], 8)
    for a in ax + [aw]:
        a[3].wait_recv()
        a[6].start()
    put_out(xs.at[qg], xm_out.at[qg], 9)
    for n, i in enumerate((2, 4, 5, 6)):
        for a in ax + [aw]:
            a[i].wait_recv()
        q = (sib % 8, qs + 1 - 2 * c, qf + 1 - 2 * c, qg + 1 - 2 * c)[n]
        put_out(xs.at[q], xm_out.at[q], 10 + n)
    steps[4].wait()
    nr_out[...] = jnp.maximum(flag_s[4], frecv[4])[0:1, 0:1].astype(I32)
    for a in ex + [ew]:
        a[3].wait_recv()
        a[6].start()
    put_out(xes.at[qg], xe_out.at[qg], 14)
    for n, i in enumerate((2, 4, 5, 6)):
        for a in ex + [ew]:
            a[i].wait_recv()
        q = (sib % 8, zn % 8 + 1 - 2 * c, yn % 8 + 1 - 2 * c, qg + 1 - 2 * c)[n]
        put_out(xes.at[q], xe_out.at[q], 15 + n)
    put_out(wms, wm_out, 19)
    put_out(wes, we_out, 20)
    for a in [aw, ew, cross] + ax + ex:
        for cp in a:
            cp.wait_send()
    for cp in outs:
        cp.wait()


def expert_kernel(own_ref, se_ref, xm_hbm, xe_hbm, wm_ref, we_ref, w1_hbm, w3_hbm, w2_hbm, pm_out, pe_out,
                  xv, wrow, rank, pv, pev, obuf, kb, startv, starts, b1, b3, b2, slots, experts, seen, ent_e, ent_u, ent_i,
                  tile_e, tile_row, tile_rank, n_tiles, wsem, xsem, osem):
    me = lax.axis_index("ep")
    n_local = w1_hbm.shape[0]
    n_main, n_ext = 8 * 128, 8 * EXT
    n_tok = n_main + n_ext
    n_blk = n_tok // 128
    xl = [pltpu.make_async_copy(xm_hbm, xv.at[pl.ds(0, n_main)], xsem.at[0]),
          pltpu.make_async_copy(xe_hbm, xv.at[pl.ds(n_main, n_ext)], xsem.at[1])]
    for cp in xl:
        cp.start()

    def clear(e, carry):
        seen[e] = 0
        return carry

    lax.fori_loop(0, NUM_EXPERTS, clear, 0)

    def listing(s, n):
        e = se_ref[me * n_local + s]
        use = (own_ref[0, e] == 1) & (seen[e] == 0)

        @pl.when(use)
        def _():
            slots[n] = s
            experts[n] = e
            seen[e] = 1
        return jnp.where(use, n + 1, n)

    n_act = lax.fori_loop(0, n_local, listing, 0)

    def fetch(i):
        s, b = slots[i], lax.rem(i, NBUF)
        return [pltpu.make_async_copy(w1_hbm.at[s], b1.at[b], wsem.at[0, b]),
                pltpu.make_async_copy(w3_hbm.at[s], b3.at[b], wsem.at[1, b]),
                pltpu.make_async_copy(w2_hbm.at[s], b2.at[b], wsem.at[2, b])]

    def start(i):
        @pl.when(i < n_act)
        def _():
            for cp in fetch(i):
                cp.start()

    for i in range(NBUF):
        start(i)

    upper = (lax.broadcasted_iota(I32, (128, 128), 0) < lax.broadcasted_iota(I32, (128, 128), 1))
    upper = upper.astype(F32).astype(BF16)
    lane = lax.broadcasted_iota(I32, (NUM_EXPERTS, 128), 1)
    code = lax.broadcasted_iota(I32, (NUM_EXPERTS, 128), 0).astype(F32) + 1.0
    run = jnp.zeros((NUM_EXPERTS, 1), F32)
    table = jnp.zeros((NUM_EXPERTS, 128), F32)
    for j in range(n_blk):
        if j < 8:
            blk = wm_ref[j]
            w = jnp.zeros((NUM_EXPERTS, 128), F32)
            for k in range(6):
                w += jnp.where(code == blk[k:k + 1, :], blk[8 + k:9 + k, :], 0.0)
        else:
            ids = jnp.concatenate([we_ref[2 * (j - 8)][:1, :EXT], we_ref[2 * (j - 8) + 1][:1, :EXT]], axis=1)
            w = jnp.where(code == ids, 1.0, 0.0)
        mask = jnp.where(w != 0.0, 1.0, 0.0)
        pos = dot(mask.astype(BF16), upper) + run
        run += jnp.sum(mask, axis=1, keepdims=True)
        table += jnp.where(lane == j + 1, run, 0.0)
        rank[j] = jnp.where(mask > 0.0, pos, -1.0)
        wrow[j] = w
    startv[...] = table.astype(I32)
    tc = pltpu.make_async_copy(startv, starts, xsem.at[2])
    tc.start()
    tc.wait()

    def list_units(i, n):
        e = experts[i]
        units = (starts[e, n_blk] + UNIT - 1) // UNIT

        def put(u, n):
            ent_e[n] = e
            ent_u[n] = u
            ent_i[n] = i
            return n + 1
        return lax.fori_loop(0, units, put, n)

    n_all = lax.fori_loop(0, n_act, list_units, 0)
    for cp in xl:
        cp.wait()

    def out_copies(j):
        if j < 8:
            return pltpu.make_async_copy(pv.at[pl.ds(j * 128, 128)], pm_out.at[pl.ds(j * 128, 128)], osem.at[j])
        return pltpu.make_async_copy(pev.at[pl.ds((j - 8) * 128, 128)], pe_out.at[pl.ds((j - 8) * 128, 128)], osem.at[j])

    def finish(j):
        if j >= 8:
            pev[(j - 8) * 128:(j - 7) * 128, :] = pv[j * 128:(j + 1) * 128, :].astype(BF16)
        out_copies(j).start()

    def flush(first, n_ent, last):
        for j in range(n_blk):
            n_tiles[j] = 0

        def list_tiles(g, carry):
            e, u = ent_e[first + g], ent_u[first + g] * UNIT
            hi = jnp.clip(starts[e, 0] - u, 0, UNIT)
            for j in range(n_blk):
                lo, hi = hi, jnp.clip(starts[e, j + 1] - u, 0, UNIT)
                k0 = lo // TILE
                some = hi > lo
                k1 = jnp.where(some, (hi - 1) // TILE + 1, k0)
                t = n_tiles[j]

                def put(k, t):
                    tile_e[j * TILES + t] = e
                    tile_row[j * TILES + t] = g * UNIT + k * TILE
                    tile_rank[j * TILES + t] = u + k * TILE

                put(k0, t)
                put(k0 + 1, t + 1)
                n_tiles[j] = t + k1 - k0

                @pl.when(k1 > k0 + 2)
                def _():
                    lax.fori_loop(2, k1 - k0, lambda k, _: put(k0 + k, t + k), None)
            return carry

        lax.fori_loop(0, n_ent, list_tiles, 0)
        for j in range(n_blk):
            n_tile = n_tiles[j]

            def one_pass(p, carry, j=j, n_tile=n_tile):
                parts = []
                for g in range(GROUP):
                    t = p * GROUP + g
                    live = t < n_tile
                    e = jnp.where(live, tile_e[j * TILES + t], 0)
                    at = jnp.where(live, tile_row[j * TILES + t], 0)
                    base = jnp.where(live, tile_rank[j * TILES + t], -1000)
                    kb[g * TILE:(g + 1) * TILE, :] = obuf[pl.ds(pl.multiple_of(at, TILE), TILE), :]
                    rows = lax.broadcasted_iota(I32, (TILE, 128), 0) + base
                    hit = rows.astype(F32) == rank[j, pl.ds(e, 1), :]
                    parts.append(jnp.where(hit, wrow[j, pl.ds(e, 1), :], 0.0))
                st = jnp.transpose(jnp.concatenate(parts, axis=0))
                res = dot(jnp.concatenate(split3(st), axis=0), kb[...])
                res = res[:128] + res[128:256] + res[256:]
                fresh = (first == 0) & (p == 0)

                @pl.when(fresh)
                def _():
                    pv[j * 128:(j + 1) * 128, :] = res

                @pl.when(jnp.logical_not(fresh))
                def _():
                    pv[j * 128:(j + 1) * 128, :] += res
                return carry

            @pl.when((first == 0) & (n_tile == 0))
            def _():
                pv[j * 128:(j + 1) * 128, :] = jnp.zeros((128, pv.shape[1]), F32)
            lax.fori_loop(0, (n_tile + GROUP - 1) // GROUP, one_pass, 0)

            @pl.when(last)
            def _():
                finish(j)

    def wait_for(k, carry):
        for cp in fetch(k):
            cp.wait()
        return carry

    def batch(bt, nxt):
        first = bt * MAXENT
        n_ent = jnp.minimum(n_all - first, MAXENT)

        def collect(q, carry):
            es = [jnp.minimum(q * 4 + g, n_ent - 1) + first for g in range(4)]
            ext = functools.reduce(jnp.logical_or, [starts[ent_e[n], n_blk] > starts[ent_e[n], 8] for n in es])

            def take(width):
                sel = []
                for n in es:
                    rows = (lax.broadcasted_iota(I32, (UNIT, 128), 0) + ent_u[n] * UNIT).astype(F32)
                    e = ent_e[n]
                    sel.append(jnp.concatenate([jnp.where(rows == rank[j, pl.ds(e, 1), :], 1.0, 0.0).astype(BF16)
                                                for j in range(width // 128)], axis=1))
                got = dot(jnp.concatenate(sel, axis=0), xv[:width, :])
                obuf[pl.ds(pl.multiple_of(q * 4 * UNIT, 4 * UNIT), 4 * UNIT), :] = got.astype(BF16)

            @pl.when(ext)
            def _():
                take(n_tok)

            @pl.when(jnp.logical_not(ext))
            def _():
                take(n_main)
            return carry

        lax.fori_loop(0, (n_ent + 3) // 4, collect, 0)

        def run_ffn(k, nxt):
            i = ent_i[first + k]

            def settle(k, carry):
                wait_for(k, carry)

                @pl.when(k < i)
                def _():
                    start(k + NBUF)
                return carry
            lax.fori_loop(nxt, i + 1, settle, 0)
            b = lax.rem(i, NBUF)
            two = (k + 1 < n_ent) & (ent_i[first + k + 1] == i)

            def ffn(n):
                rows = pl.ds(pl.multiple_of(k * UNIT, UNIT), n)
                xg = obuf[rows, :]
                act = (jax.nn.silu(dot(xg, b1[b])) * dot(xg, b3[b])).astype(BF16)
                obuf[rows, :] = dot(act, b2[b]).astype(BF16)

            @pl.when(two)
            def _():
                ffn(2 * UNIT)

            @pl.when(jnp.logical_not(two))
            def _():
                ffn(UNIT)
            end = k + jnp.where(two, 2, 1)

            @pl.when((first + end == n_all) | (ent_i[first + end] != i))
            def _():
                start(i + NBUF)
            return end, jnp.maximum(nxt, i + 1)

        nxt = lax.while_loop(lambda s: s[0] < n_ent, lambda s: run_ffn(*s), (0, nxt))[1]
        flush(first, n_ent, first + n_ent == n_all)
        return nxt

    nxt = lax.fori_loop(0, (n_all + MAXENT - 1) // MAXENT, batch, 0)

    def drain(k, carry):
        wait_for(k, carry)
        start(k + NBUF)
        return carry

    lax.fori_loop(nxt, n_act, drain, 0)

    @pl.when(n_all == 0)
    def _():
        pv[...] = jnp.zeros_like(pv)
        for j in range(n_blk):
            finish(j)
    for j in range(n_blk):
        out_copies(j).wait()


def scatter_kernel(pm_hbm, pe_hbm, z_ref, gw_ref, y_ref,
                   out_ref, mo, md, mrg, mrf, mrs, mfin, eo, ed, erg, erf, ers, gsib, ecr, ssem, rsem, lsem):
    me, c, h, sib, yn, zn, mir, first, second, diag = dims()
    cols = mo.shape[-1]
    mine = pl.ds(pl.multiple_of(c * cols, 128), cols)
    theirs = pl.ds(pl.multiple_of((1 - c) * cols, 128), cols)
    local, peer = [], []
    for base, (src, own, got, chips, swap) in ((0, (pe_hbm, eo, ed, (diag, yn, zn, me), (0, 1, 2, 3))),
                                               (4, (pm_hbm, mo, md, (diag, first, second, me), (0, 2, 1, 3)))):
        for i in range(4):
            rows = pl.ds(2 * ((chips[i] % 8) // 2), 2)
            sib_rows = pl.ds(2 * ((chips[swap[i]] % 8) // 2), 2)
            local.append(pltpu.make_async_copy(src.at[rows, :, mine], own.at[i], lsem.at[base + i]))
            peer.append(pltpu.make_async_remote_copy(
                src_ref=src.at[sib_rows, :, theirs], dst_ref=got.at[i], send_sem=ssem.at[base + i],
                recv_sem=rsem.at[base + i], device_id={"ep": sib}, device_id_type=MESH))
    for i in (0, 4, 1, 5, 2, 6, 3, 7):
        local[i].start()
    barrier([{"ep": sib}, {"ep": yn}, {"ep": zn}, {"ep": mir}])
    for i in (0, 4, 1, 5, 2, 6, 3, 7):
        peer[i].start()

    def rcopy(src, dst, i, dev):
        return pltpu.make_async_remote_copy(src_ref=src, dst_ref=dst, send_sem=ssem.at[i], recv_sem=rsem.at[i],
                                            device_id={"ep": dev}, device_id_type=MESH)

    eg, ef, es = rcopy(eo.at[0], erg, 8, yn), rcopy(eo.at[1], erf, 9, yn), rcopy(eo.at[2], ers, 10, zn)
    back = rcopy(eo.at[3], ecr, 11, mir)
    gshare = rcopy(gw_ref, gsib, 12, sib)
    order = (1 - c, c)
    mg = [rcopy(mo.at[0, b], mrg.at[b], 13 + n, first) for n, b in enumerate(order)]
    ms = [rcopy(mo.at[2, b], mrs.at[b], 15 + n, second) for n, b in enumerate(order)]
    mf = rcopy(mo.at[1], mrf, 17, first)
    mfinal = rcopy(mo.at[3, 1 - c], mfin, 18, sib)

    def joined(own, got, i, base):
        local[base + i].wait()
        peer[base + i].wait_recv()
        own[i] = own[i] + got[i]

    joined(eo, ed, 0, 0)
    eg.start()
    joined(mo, md, 0, 4)
    mg[0].start()
    joined(eo, ed, 1, 0)
    ef.start()
    mg[1].start()
    joined(eo, ed, 2, 0)
    joined(eo, ed, 3, 0)
    gshare.start()
    eg.wait_recv()
    eo[2] = eo[2] + erg[...]
    es.start()
    joined(mo, md, 1, 4)
    mf.start()
    joined(mo, md, 2, 4)
    mg[0].wait_recv()
    mo[2, 1 - c] = mo[2, 1 - c] + mrg[1 - c]
    ms[0].start()
    ef.wait_recv()
    es.wait_recv()
    eo[3] = eo[3] + erf[...] + ers[...]
    back.start()
    joined(mo, md, 3, 4)
    out_ref[...] = z_ref[...]
    mg[1].wait_recv()
    mo[2, c] = mo[2, c] + mrg[c]
    ms[1].start()
    mf.wait_recv()
    mo[3] = mo[3] + mrf[...]
    gshare.wait_recv()
    back.wait_recv()
    for b, g in ((c, gw_ref), (1 - c, gsib)):
        for part in split3(g[...]):
            mo[3, b] += dot(part, ecr[b], 0, 0)
    ms[0].wait_recv()
    mo[3, 1 - c] = mo[3, 1 - c] + mrs[1 - c]
    mfinal.start()
    ms[1].wait_recv()
    out_ref[:, mine] += mo[3, c] + mrs[c]
    mfinal.wait_recv()
    out_ref[:, theirs] += mfin[...]
    y_ref[...] = out_ref[...].astype(y_ref.dtype)
    for cp in peer + mg + ms + [eg, ef, es, back, gshare, mf, mfinal]:
        cp.wait_send()


def solution(mesh):
    any_space = pl.BlockSpec(memory_space=pl.ANY)
    vmem = pl.BlockSpec(memory_space=pltpu.VMEM)
    smem = pl.BlockSpec(memory_space=pltpu.SMEM)
    sds = jax.ShapeDtypeStruct

    def gather(x, at, se, rnd, wr, w1, w3, w2):
        d, ff = w1.shape
        return pl.pallas_call(
            gather_kernel,
            out_shape=(sds((8, 128, d), BF16), sds((8, EXT, d), BF16), sds((8, 16, 128), F32),
                       sds((8, 8, 128), F32), sds((8, 128), I32), sds((EXT, 128), F32),
                       sds((128, d), F32), sds((1, 1), I32)),
            in_specs=[vmem, vmem, vmem, smem, vmem] + [any_space] * 3,
            out_specs=(any_space,) * 4 + (vmem,) * 4,
            scratch_shapes=[
                pltpu.VMEM((8, 128, d), BF16), pltpu.VMEM((8, EXT, d), BF16),
                pltpu.VMEM((8, 16, 128), F32), pltpu.VMEM((8, 8, 128), F32),
                pltpu.VMEM((EXT, d), BF16), pltpu.VMEM((8, 128), F32),
                pltpu.VMEM((EXT, d), BF16), pltpu.VMEM((8, 128), F32), pltpu.VMEM((16, 128), F32),
                pltpu.VMEM((2, NUM_EXPERTS, 128), F32), pltpu.VMEM((NUM_EXPERTS, 128), F32),
                pltpu.VMEM((5, 8, 128), F32), pltpu.VMEM((5, 8, 128), F32),
                pltpu.VMEM((d, ff), BF16), pltpu.VMEM((d, ff), BF16), pltpu.VMEM((ff, d), BF16),
                pltpu.SemaphoreType.DMA((60,)), pltpu.SemaphoreType.DMA((60,)), pltpu.SemaphoreType.DMA((21,)),
            ],
            compiler_params=pltpu.CompilerParams(collective_id=0, has_side_effects=True),
            name="gather_rows",
        )(x, at, se, rnd, wr, w1, w3, w2)

    def experts(own, se, xm, xe, wm, we, w1, w3, w2):
        _, d, ff = w1.shape
        n_tok = 8 * (128 + EXT)
        return pl.pallas_call(
            expert_kernel,
            out_shape=(sds((8 * 128, d), F32), sds((8 * EXT, d), BF16)),
            in_specs=[smem, smem, any_space, any_space, vmem, vmem] + [any_space] * 3,
            out_specs=(any_space, any_space),
            scratch_shapes=[
                pltpu.VMEM((n_tok, d), BF16), pltpu.VMEM((n_tok // 128, NUM_EXPERTS, 128), F32), pltpu.VMEM((n_tok // 128, NUM_EXPERTS, 128), F32),
                pltpu.VMEM((n_tok, d), F32), pltpu.VMEM((8 * EXT, d), BF16), pltpu.VMEM((MAXENT * UNIT, d), BF16),
                pltpu.VMEM((GROUP * TILE, d), BF16),
                pltpu.VMEM((NUM_EXPERTS, 128), I32), pltpu.SMEM((NUM_EXPERTS, 128), I32),
                pltpu.VMEM((NBUF, d, ff), BF16), pltpu.VMEM((NBUF, d, ff), BF16), pltpu.VMEM((NBUF, ff, d), BF16),
                pltpu.SMEM((32,), I32), pltpu.SMEM((32,), I32), pltpu.SMEM((NUM_EXPERTS,), I32),
                pltpu.SMEM((384,), I32), pltpu.SMEM((384,), I32), pltpu.SMEM((384,), I32),
                pltpu.SMEM((12 * TILES,), I32), pltpu.SMEM((12 * TILES,), I32), pltpu.SMEM((12 * TILES,), I32),
                pltpu.SMEM((16,), I32),
                pltpu.SemaphoreType.DMA((3, NBUF)), pltpu.SemaphoreType.DMA((3,)), pltpu.SemaphoreType.DMA((12,)),
            ],
            name="expert_rows",
        )(own, se, xm, xe, wm, we, w1, w3, w2)

    def scatter(pm, pe, z, gw, last):
        d = z.shape[1]
        half = d // 2
        big, small = (2, 128, half), (2, EXT, half)
        return pl.pallas_call(
            scatter_kernel,
            out_shape=sds((128, d), F32),
            in_specs=[any_space, any_space, vmem, vmem],
            out_specs=vmem,
            scratch_shapes=[
                pltpu.VMEM((128, d), F32),
                pltpu.VMEM((4,) + big, F32), pltpu.VMEM((4,) + big, F32),
                pltpu.VMEM(big, F32), pltpu.VMEM(big, F32), pltpu.VMEM(big, F32), pltpu.VMEM((128, half), F32),
                pltpu.VMEM((4,) + small, BF16), pltpu.VMEM((4,) + small, BF16),
                pltpu.VMEM(small, BF16), pltpu.VMEM(small, BF16), pltpu.VMEM(small, BF16), pltpu.VMEM((EXT, 128), F32),
                pltpu.VMEM(small, BF16),
                pltpu.SemaphoreType.DMA((20,)), pltpu.SemaphoreType.DMA((20,)), pltpu.SemaphoreType.DMA((8,)),
            ],
            compiler_params=pltpu.CompilerParams(collective_id=1 if last else 2, has_side_effects=True),
            name="scatter_sums" if last else "scatter_more",
        )(pm, pe, z, gw)

    def device_step(x, slot_expert, w1, w3, w2, assign, wr, w1s, w3s, w2s):
        d = x.shape[1]
        rows_of = lambda a: a.reshape(-1, d)

        def gathered(r):
            return gather(x, assign.T, slot_expert, r.reshape(1), wr.T, w1s, w3s, w2s)

        def summed(parts):
            xm, xe, wm, we, own = parts
            pm, pe = experts(own, slot_expert, rows_of(xm), rows_of(xe), wm, we, w1, w3, w2)
            return pm.reshape(8, 128, d), pe.reshape(8, EXT, d)

        def again(carry):
            r, n, z = carry
            *parts, gw, _, _ = gathered(r)
            return r + 1, n, scatter(*summed(parts), z, gw, False)

        *parts, gw, z, nr = gathered(jnp.int32(0))
        z = lax.while_loop(lambda s: s[0] < s[1], again, (jnp.int32(1), nr.reshape(()), z))[2]
        return scatter(*summed(parts), z, gw, True).astype(BF16)

    tok = P(("dp", "ep"), None)
    slot = P("ep", None, None)
    return jax.shard_map(device_step, mesh=mesh,
                         in_specs=(tok, P(), slot, slot, slot, tok, P(), P(), P(), P()),
                         out_specs=tok, check_vma=False)
```

time: 157 us -> 112 us (0.71)
  Pallas kernels: 150 us -> 110 us
  local copies, waits for them, and re-layouts: 5.28 us -> 0.02 us
    pallas_call x1, Pallas kernels: 50.9 us -> 26.6 us  [experts(): pl.pallas_call(expert_kernel, out_shape=(sds((8 * 128, d), F32), sds((8 *...]
    pallas_call x1, Pallas kernels: 58.8 us -> 43.8 us  [scatter(): pl.pallas_call(scatter_kernel, out_shape=sds((128, d), F32), in_specs=[an...]
    while x4 -> x0, local copies, waits for them, and re-layouts: 2.03 us -> none  [the longest x1 1.15 us: device_step(): out = lax.while_loop(lambda s: s[0] < s[1], body, carry)[2]]
where the time goes in v2:
time: 112 us
  Pallas kernels  110 us (98%)
  other arithmetic  1.92 us (2%)
    pallas_call x1, Pallas kernels, scatter(): pl.pallas_call(scatter_kernel, out_shape=sds((128, d), F32), in_specs=[an...  43.8 us
    pallas_call x1, Pallas kernels, gather(): pl.pallas_call(gather_kernel, out_shape=(sds((8, 128, d), BF16), sds((8,...  39.2 us
    pallas_call x1, Pallas kernels, experts(): pl.pallas_call(expert_kernel, out_shape=(sds((8 * 128, d), F32), sds((8 *...  26.6 us

profile of v2, /device:TPU:0, one launch (start us, length us, event | category | flops | bytes accessed | tf_op | source)
XLA Modules:
  0.0 112.4 jit_solution(16213890969916631883)
XLA Ops:
  0.0 0.0 copy-start
  0.0 0.0 copy-start.2
  0.0 0.0 copy-start.3
  0.0 0.0 copy-start.4
  0.0 39.2 %gather_rows.2 = (bf16[8,128,1536]{2,1,0:T(8,128)(2,1)}, bf16[8,64,1536]{2,1,0:T(8,128)(2,1)}, f32[8,16,128]{2,1,0:T(8,128)}, f32[8,8,128]{2,1,0:T(8,128)}, s32[...) custom-call(bf16[128,1536]{1,0:T(8,128)(2,1)} %x_ref.1, s32[6,128]{1,0:T(8,128)} %bitcast.38, ...), custom_call_target="tpu_custom_call" | custom-call | tf_op jit(solution)/shard_map/gather_rows/pallas_call | solution.py:615
  39.2 0.0 copy-done
  39.2 0.0 copy-done.2
  39.2 0.0 copy-done.3
  39.2 0.0 copy-done.4
  39.3 0.8 while.10
  40.1 0.0 copy-start.1
  40.1 26.6 %expert_rows.2 = (f32[1024,1536]{1,0:T(8,128)}, bf16[512,1536]{1,0:T(8,128)(2,1)}) custom-call(s32[8,128]{1,0:T(8,128)} %get-tuple-element.91.own_ref, s32[320]{0:T(512)S(1)} %get-tuple-element.269, bf16[1024,1536]{1,0:T(8,128)(2,1)} %bitcast.35, bf16[512,1536]{1,0:T(8,128)(2,1)} %bitcast.37, f32[8,16,128]{2,1,0:T(8,128)} %get-tuple-element.94.wm_ref, ...), custom_call_target="tpu_custom_call" | custom-call | tf_op jit(solution)/shard_map/expert_rows/pallas_call | solution.py:639
  66.7 0.0 copy-done.1
  66.7 43.8 %scatter_sums.1 = f32[128,1536]{1,0:T(8,128)} custom-call(f32[8,128,1536]{2,1,0:T(8,128)} %bitcast.34, bf16[8,64,1536]{2,1,0:T(8,128)(2,1)} %bitcast.36, f32[128,1536]{1,0:T(8,128)S(1)} %copy-done.1, f32[64,128]{1,0:T(8,128)} %get-tuple-element.101.gw_ref), custom_call_target="tpu_custom_call" | custom-call | tf_op jit(solution)/shard_map/scatter_sums/pallas_call | solution.py:663
  110.5 1.9 %convert_element_type.3 = bf16[128,1536]{1,0:T(8,128)(2,1)} convert(f32[128,1536]{1,0:T(8,128)} %scatter_sums.1) | non-fusion elementwise | flops 196608 | bytes 1179648 | tf_op jit(solution)/shard_map/convert_element_type | solution.py:700
Async XLA Ops:
  0.0 39.2 %copy-start = (bf16[1536,1024]{1,0:T(8,128)(2,1)S(1)}, bf16[1536,1024]{1,0:T(8,128)(2,1)}, u32[]{:S(2)}) copy-start(bf16[1536,1024]{1,0:T(8,128)(2,1)} %w1_hbm.2) | copy-start | bytes 9437188
  0.0 39.2 %copy-start.2 = (bf16[128,1536]{1,0:T(8,128)(2,1)S(1)}, bf16[128,1536]{1,0:T(8,128)(2,1)}, u32[]{:S(2)}) copy-start(bf16[128,1536]{1,0:T(8,128)(2,1)} %x_ref.1) | copy-start | bytes 1179652
  0.0 39.2 %copy-start.3 = (s32[320]{0:T(512)S(1)}, s32[320]{0:T(512)}, u32[]{:S(2)}) copy-start(s32[320]{0:T(512)} %se_ref.3) | copy-start | bytes 3844
  0.0 39.2 %copy-start.4 = (s32[128,6]{0,1:T(8,128)S(1)}, s32[128,6]{0,1:T(8,128)}, u32[]{:S(2)}) copy-start(s32[128,6]{0,1:T(8,128)} %param.17) | copy-start | bytes 9220
  40.1 26.6 %copy-start.1 = (f32[128,1536]{1,0:T(8,128)S(1)}, f32[128,1536]{1,0:T(8,128)}, u32[]{:S(2)}) copy-start(f32[128,1536]{1,0:T(8,128)} %get-tuple-element.100.z_ref) | copy-start | bytes 2359300

commit v3 on v2

v3 whole, which is shorter than its diff:
```python
import functools

import jax
import jax.numpy as jnp
from jax import lax
from jax.experimental import pallas as pl
from jax.experimental.pallas import tpu as pltpu
from jax.sharding import PartitionSpec as P

ROUTE_SCALE = 2.5
LANES, PEERS, CHIPS = 128, 8, 4
ZERO, ONE = 0.0, 1.0
MESH = pl.DeviceIdType.MESH
NUM_EXPERTS = 64
EXT = 64
UNIT = LANES
PIECES = 2
NBUF = 6
MAXENT = 15
GROUP = 16
TILES = 160
TILE_BITS = CHIPS
TILE = 1 << TILE_BITS
TAKE = 3
F32, BF16, I32 = jnp.float32, jnp.bfloat16, jnp.int32


def dims():
    me = lax.axis_index("ep")
    c, y, z, h = me % 2, (me // 2) % 2, (me // CHIPS) % 2, me // PEERS
    sib = me + 1 - 2 * c
    yn = me + 2 - CHIPS * y
    zn = me + CHIPS - PEERS * z
    mir = me + PEERS - 16 * h
    first = yn + c * (zn - yn)
    second = zn + c * (yn - zn)
    diag = yn + zn - me
    return me, c, h, sib, yn, zn, mir, first, second, diag


def barrier(peers):
    sem = pltpu.get_barrier_semaphore()
    for peer in peers:
        pl.semaphore_signal(sem, inc=1, device_id=peer, device_id_type=MESH)
    pl.semaphore_wait(sem, len(peers))


def dot(a, b, ca=1, cb=0):
    return lax.dot_general(a, b, (((ca,), (cb,)), ((), ())), preferred_element_type=F32)


def split3(v):
    hi = v.astype(BF16)
    rest = v - hi.astype(F32)
    mid = rest.astype(BF16)
    lo = (rest - mid.astype(F32)).astype(BF16)
    return hi, mid, lo


def gather_kernel(x_ref, at_ref, se_ref, rnd_ref, wr_ref, w1_hbm, w3_hbm, w2_hbm,
                  xm_out, xe_out, wm_out, we_out, own_out, gw_out, z_out, nr_out,
                  xs, xes, wms, wes, xcr, ecr, xsnd, esnd, wsnd, cand_s, own_s, flag_s, frecv,
                  w1s, w3s, w2s, ssem, rsem, lsem):
    me, c, h, sib, yn, zn, mir, first, second, diag = dims()
    dp = lax.axis_index("dp")
    qm, qf, qs, qg = me % PEERS, first % PEERS, second % PEERS, diag % PEERS
    loads = [pltpu.make_async_copy(a, b, lsem.at[i]) for i, (a, b) in
             enumerate(((w1_hbm, w1s), (w3_hbm, w3s), (w2_hbm, w2s)))]
    for cp in loads:
        cp.start()
    barrier([{"ep": sib}, {"ep": yn}, {"ep": zn}, {"ep": mir}, {"dp": 1 - dp}])

    def rcopy(src, dst, i, dev):
        return pltpu.make_async_remote_copy(src_ref=src, dst_ref=dst, send_sem=ssem.at[i], recv_sem=rsem.at[i],
                                            device_id=dev, device_id_type=MESH)

    def spread(own, buf, base, one, two):
        ep = lambda d: {"ep": d}
        q1, q2 = one % PEERS, two % PEERS
        return [rcopy(own, buf.at[qm], base, ep(one)), rcopy(own, buf.at[qm], base + 1, ep(two)),
                rcopy(own, buf.at[qm], base + 2, ep(sib)), rcopy(buf.at[q1], buf.at[q1], base + 3, ep(two)),
                rcopy(buf.at[q1], buf.at[q1], base + CHIPS, ep(sib)), rcopy(buf.at[q2], buf.at[q2], base + 5, ep(sib)),
                rcopy(buf.at[qg], buf.at[qg], base + 6, ep(sib))]

    parts = [pl.ds(i * (x_ref.shape[0] // PIECES), x_ref.shape[0] // PIECES) for i in range(PIECES)]
    ax = [spread(x_ref.at[r], xs.at[:, r], 45 + 7 * i, first, second) for i, r in enumerate(parts)]
    for i in range(2):
        ax[0][i].start()

    n_tok = x_ref.shape[0]
    n_slots = se_ref.shape[0]
    rnd = jnp.full((1, 1), rnd_ref[0], I32).astype(F32)
    first_round = jnp.where(rnd == ZERO, ONE, ZERO)
    expert_of = se_ref[...].reshape(1, n_slots)
    eye = (lax.broadcasted_iota(I32, (NUM_EXPERTS, n_slots), 0) == expert_of).astype(F32)
    eye_bf = eye.astype(BF16)
    lane_slot = lax.broadcasted_iota(I32, (1, n_slots), 1)
    per_half = n_slots // 2
    here = jnp.where((lane_slot >= h * per_half) & (lane_slot < (h + 1) * per_half), ONE, ZERO)
    avail = jnp.where(jnp.sum(eye * here, axis=1, keepdims=True) > ZERO, ONE, ZERO)
    row_slot = lax.broadcasted_iota(I32, (n_slots, n_tok), 0)
    hot = jnp.concatenate([(row_slot == at_ref[k:k + 1, :]).astype(F32).astype(BF16) for k in range(6)], axis=1)
    picks_all = dot(eye_bf, hot)
    picks = [picks_all[:, k * n_tok:(k + 1) * n_tok] for k in range(6)]
    code = lax.broadcasted_iota(I32, (NUM_EXPERTS, n_tok), 0).astype(F32) + ONE
    ids = [jnp.sum(p * code, axis=0, keepdims=True) for p in picks]
    miss = [jnp.sum(p * (ONE - avail), axis=0, keepdims=True) for p in picks]
    none = jnp.zeros((2, n_tok), F32)
    id_all = jnp.concatenate(ids + [none], axis=0)
    miss_all = jnp.concatenate(miss + [none], axis=0)

    upper = (lax.broadcasted_iota(I32, (n_tok, n_tok), 0) < lax.broadcasted_iota(I32, (n_tok, n_tok), 1))
    before = dot(miss_all.astype(BF16), upper.astype(F32).astype(BF16))
    offset = -EXT * rnd
    count = jnp.zeros((1, 1), F32)
    row_ext = lax.broadcasted_iota(I32, (EXT, n_tok), 0).astype(F32)
    sels = []
    for k in range(6):
        sels.append(jnp.where((row_ext == before[k:k + 1, :] + offset) & (miss[k] > ZERO), ONE, ZERO))
        mk = jnp.sum(miss[k], axis=1, keepdims=True)
        offset += mk
        count += mk
    take = functools.reduce(lambda a, b: a + b, sels)
    xsnd[...] = dot(take.astype(BF16), x_ref[...]).astype(BF16)
    piece = [pl.ds(i * (EXT // PIECES), EXT // PIECES) for i in range(PIECES)]
    cross = [rcopy(xsnd.at[r], xcr.at[r], 20 + i, {"ep": mir}) for i, r in enumerate(piece)]
    cross.append(rcopy(esnd, ecr, 19, {"ep": mir}))
    for cp in cross[:-1]:
        cp.start()
    codes = jnp.zeros((PEERS, EXT), F32)
    for k in range(6):
        codes += dot(jnp.broadcast_to(ids[k], (PEERS, n_tok)).astype(BF16), sels[k].astype(BF16), 1, 1)
    esnd[...] = jnp.concatenate([codes, jnp.zeros((PEERS, LANES - EXT), F32)], axis=1)
    cross[-1].start()
    for a in ax[1:]:
        for i in range(2):
            a[i].start()
    for a in ax:
        a[2].start()

    gate = jax.nn.sigmoid(dot(wr_ref[...], x_ref[...], 1, 1))
    picked = gate * functools.reduce(lambda a, b: a + b, picks)
    total = jnp.sum(picked, axis=0, keepdims=True)
    weight = ROUTE_SCALE * picked / jnp.maximum(total, 1e-30)
    wk = [jnp.sum(p * weight, axis=0, keepdims=True) for p in picks]
    w_all = jnp.concatenate(wk + [none], axis=0) * (ONE - miss_all) * first_round
    packed = jnp.concatenate([id_all, w_all], axis=0)
    wsnd[...] = packed
    wms[qm] = packed
    aw = spread(wsnd, wms, 7, first, second)
    for i in range(3):
        aw[i].start()
    gw_out[...] = functools.reduce(lambda a, b: a + b, [sel * w for sel, w in zip(sels, wk)])
    flag_s[0] = jnp.broadcast_to(jnp.floor((count + (EXT - 1)) * (ONE / EXT)), (PEERS, LANES))
    steps = [rcopy(flag_s.at[i], frecv.at[i], 14 + i, d) for i, d in
             enumerate(({"dp": 1 - dp}, {"ep": sib}, {"ep": mir}, {"ep": zn}, {"ep": yn}))]
    steps[0].start()

    def vote(i):
        steps[i].wait()
        flag_s[i + 1] = jnp.maximum(flag_s[i], frecv[i])
        steps[i + 1].start()

    outs = []

    def put_out(src, dst, i):
        outs.append(pltpu.make_async_copy(src, dst, lsem.at[i]))
        outs[-1].start()

    put_out(x_ref, xm_out.at[qm], 3)

    slot_row = lax.broadcasted_iota(I32, (n_slots, LANES), 0)
    lane_dev = lax.broadcasted_iota(I32, (n_slots, LANES), 1)
    lo = (lane_dev + PEERS * h) * (n_slots // 16)
    block = ((slot_row >= lo) & (slot_row < lo + n_slots // 16) & (lane_dev < PEERS)).astype(F32).astype(BF16)
    cand = jnp.where(dot(eye_bf, block) > ZERO, ONE, ZERO)
    several = jnp.where(jnp.sum(cand, axis=1, keepdims=True) > ONE, ONE, ZERO)
    lane = lax.broadcasted_iota(I32, (1, LANES), 1).astype(F32)
    block_key = jnp.where(cand > ZERO, jnp.broadcast_to(lane, cand.shape), 1e9)
    cand_s[0] = block_key
    there = jnp.where(jnp.sum(eye * (ONE - here), axis=1, keepdims=True) > ZERO, ONE, 2.0)
    cand_s[1] = jnp.broadcast_to(several * there, cand.shape)
    load0 = jnp.sum(cand * (ONE - several) * there, axis=0, keepdims=True)

    def pick(e, load):
        key = cand_s[0, pl.ds(e, 1), :] + load * 256.0
        best = jnp.min(key, axis=1, keepdims=True)
        sel = jnp.where((key == best) & (key < 1e8), ONE, ZERO)
        own_s[pl.ds(e, 1), :] = sel
        return load + sel * cand_s[1, pl.ds(e, 1), :]

    load1 = lax.fori_loop(0, NUM_EXPERTS // 2, pick, load0)
    vote(0)

    for a in ax + [aw]:
        a[0].wait_recv()
        a[3].start()
        a[CHIPS].start()
    for a in ax + [aw]:
        a[1].wait_recv()
        a[5].start()
    put_out(xs.at[qf], xm_out.at[qf], CHIPS)
    put_out(xs.at[qs], xm_out.at[qs], 5)
    vote(1)
    lax.fori_loop(NUM_EXPERTS // 2, NUM_EXPERTS, pick, load1)
    mine = jnp.where(lax.broadcasted_iota(I32, (PEERS, LANES), 1) == qm, ONE, ZERO)
    own = dot(mine.astype(BF16), own_s[...].astype(BF16), 1, 1)
    own_out[...] = jnp.concatenate([own, jnp.zeros((PEERS, LANES - NUM_EXPERTS), F32)], axis=1).astype(I32)
    vote(2)

    ew = spread(ecr, wes, 24, zn, yn)
    ex = [spread(xcr.at[r], xes.at[:, r], 31 + 7 * i, zn, yn) for i, r in enumerate(piece)]
    for i, a in enumerate(ex):
        cross[i].wait_recv()
        for n in range(3):
            a[n].start()
    cross[-1].wait_recv()
    wes[qm] = ecr[...]
    for n in range(3):
        ew[n].start()
    put_out(xcr, xe_out.at[qm], 6)
    vote(3)

    for cp in loads:
        cp.wait()
    hg = dot(x_ref[...], w1s[...])
    hu = dot(x_ref[...], w3s[...])
    act = (jax.nn.silu(hg) * hu).astype(BF16)
    z_out[...] = dot(act, w2s[...]) * first_round

    for a in ex + [ew]:
        a[0].wait_recv()
        a[3].start()
        a[CHIPS].start()
    for a in ex + [ew]:
        a[1].wait_recv()
        a[5].start()
    put_out(xes.at[zn % PEERS], xe_out.at[zn % PEERS], 7)
    put_out(xes.at[yn % PEERS], xe_out.at[yn % PEERS], PEERS)
    for a in ax + [aw]:
        a[3].wait_recv()
        a[6].start()
    put_out(xs.at[qg], xm_out.at[qg], 9)
    for n, i in enumerate((2, CHIPS, 5, 6)):
        for a in ax + [aw]:
            a[i].wait_recv()
        q = (sib % PEERS, qs + 1 - 2 * c, qf + 1 - 2 * c, qg + 1 - 2 * c)[n]
        put_out(xs.at[q], xm_out.at[q], 10 + n)
    steps[CHIPS].wait()
    nr_out[...] = jnp.maximum(flag_s[CHIPS], frecv[CHIPS])[0:1, 0:1].astype(I32)
    for a in ex + [ew]:
        a[3].wait_recv()
        a[6].start()
    put_out(xes.at[qg], xe_out.at[qg], 14)
    for n, i in enumerate((2, CHIPS, 5, 6)):
        for a in ex + [ew]:
            a[i].wait_recv()
        q = (sib % PEERS, zn % PEERS + 1 - 2 * c, yn % PEERS + 1 - 2 * c, qg + 1 - 2 * c)[n]
        put_out(xes.at[q], xe_out.at[q], 15 + n)
    put_out(wms, wm_out, 19)
    put_out(wes, we_out, 20)
    for a in [aw, ew, cross] + ax + ex:
        for cp in a:
            cp.wait_send()
    for cp in outs:
        cp.wait()


def expert_kernel(own_ref, se_ref, xm_hbm, xe_hbm, wm_ref, we_ref, w1_hbm, w3_hbm, w2_hbm, pm_out, pe_out,
                  xv, wrow, rank, pv, pev, obuf, kb, startv, starts, b1, b3, b2, slots, experts, seen, ent_e, ent_u, ent_i,
                  tile_e, tile_row, tile_rank, n_tiles, wsem, xsem, osem):
    me = lax.axis_index("ep")
    n_local = w1_hbm.shape[0]
    n_main, n_ext = PEERS * LANES, PEERS * EXT
    n_tok = n_main + n_ext
    n_blk = n_tok // LANES
    xl = [pltpu.make_async_copy(xm_hbm, xv.at[pl.ds(0, n_main)], xsem.at[0]),
          pltpu.make_async_copy(xe_hbm, xv.at[pl.ds(n_main, n_ext)], xsem.at[1])]
    for cp in xl:
        cp.start()

    def clear(e, carry):
        seen[e] = 0
        return carry

    lax.fori_loop(0, NUM_EXPERTS, clear, 0)

    def listing(s, n):
        e = se_ref[me * n_local + s]
        use = (own_ref[0, e] == 1) & (seen[e] == 0)

        @pl.when(use)
        def _():
            slots[n] = s
            experts[n] = e
            seen[e] = 1
        return jnp.where(use, n + 1, n)

    n_act = lax.fori_loop(0, n_local, listing, 0)

    def fetch(i):
        s, b = slots[i], lax.rem(i, NBUF)
        return [pltpu.make_async_copy(w1_hbm.at[s], b1.at[b], wsem.at[0, b]),
                pltpu.make_async_copy(w3_hbm.at[s], b3.at[b], wsem.at[1, b]),
                pltpu.make_async_copy(w2_hbm.at[s], b2.at[b], wsem.at[2, b])]

    def start(i):
        @pl.when(i < n_act)
        def _():
            for cp in fetch(i):
                cp.start()

    for i in range(NBUF):
        start(i)

    upper = (lax.broadcasted_iota(I32, (LANES, LANES), 0) < lax.broadcasted_iota(I32, (LANES, LANES), 1))
    upper = upper.astype(F32).astype(BF16)
    lane = lax.broadcasted_iota(I32, (NUM_EXPERTS, LANES), 1)
    code = lax.broadcasted_iota(I32, (NUM_EXPERTS, LANES), 0).astype(F32) + ONE
    run = jnp.zeros((NUM_EXPERTS, 1), F32)
    table = jnp.zeros((NUM_EXPERTS, LANES), F32)
    for j in range(n_blk):
        if j < PEERS:
            blk = wm_ref[j]
            w = jnp.zeros((NUM_EXPERTS, LANES), F32)
            for k in range(6):
                w += jnp.where(code == blk[k:k + 1, :], blk[PEERS + k:9 + k, :], ZERO)
        else:
            ids = jnp.concatenate([we_ref[2 * (j - PEERS)][:1, :EXT], we_ref[2 * (j - PEERS) + 1][:1, :EXT]], axis=1)
            w = jnp.where(code == ids, ONE, ZERO)
        mask = jnp.where(w != ZERO, ONE, ZERO)
        pos = dot(mask.astype(BF16), upper) + run
        run += jnp.sum(mask, axis=1, keepdims=True)
        table += jnp.where(lane == j + 1, run, ZERO)
        rank[j] = jnp.where(mask > ZERO, pos, -ONE)
        wrow[j] = w
    startv[...] = table.astype(I32)
    tc = pltpu.make_async_copy(startv, starts, xsem.at[2])
    tc.start()
    tc.wait()

    def list_units(i, n):
        e = experts[i]
        units = (starts[e, n_blk] + UNIT - 1) >> 7

        def put(u, n):
            ent_e[n] = e
            ent_u[n] = u
            ent_i[n] = i
            return n + 1
        return lax.fori_loop(0, units, put, n)

    n_all = lax.fori_loop(0, n_act, list_units, 0)
    for cp in xl:
        cp.wait()

    def out_copies(j):
        if j < PEERS:
            return pltpu.make_async_copy(pv.at[pl.ds(j * LANES, LANES)], pm_out.at[pl.ds(j * LANES, LANES)], osem.at[j])
        return pltpu.make_async_copy(pev.at[pl.ds((j - PEERS) * LANES, LANES)], pe_out.at[pl.ds((j - PEERS) * LANES, LANES)], osem.at[j])

    def finish(j):
        if j >= PEERS:
            pev[(j - PEERS) * LANES:(j - 7) * LANES, :] = pv[j * LANES:(j + 1) * LANES, :].astype(BF16)
        out_copies(j).start()

    def flush(first, n_ent, last):
        for j in range(n_blk):
            n_tiles[j] = 0

        def list_tiles(g, carry):
            e, u = ent_e[first + g], ent_u[first + g] * UNIT
            def span(blocks, hi):
                for j in blocks:
                    lo, hi = hi, jnp.clip(starts[e, j + 1] - u, 0, UNIT)
                    k0 = lo >> TILE_BITS
                    k1 = jnp.where(hi > lo, ((hi - 1) >> TILE_BITS) + 1, k0)
                    t = n_tiles[j]

                    def put(k, t, j=j):
                        tile_e[j * TILES + t] = e
                        tile_row[j * TILES + t] = g * UNIT + k * TILE
                        tile_rank[j * TILES + t] = u + k * TILE

                    put(k0, t)
                    put(k0 + 1, t + 1)
                    n_tiles[j] = t + k1 - k0

                    @pl.when(k1 > k0 + 2)
                    def _():
                        lax.fori_loop(2, k1 - k0, lambda k, _: put(k0 + k, t + k), None)

            span(range(PEERS), jnp.clip(-u, 0, UNIT))

            @pl.when(starts[e, n_blk] > starts[e, PEERS])
            def _():
                span(range(PEERS, n_blk), jnp.clip(starts[e, PEERS] - u, 0, UNIT))
            return carry

        lax.fori_loop(0, n_ent, list_tiles, 0)
        for j in range(n_blk):
            n_tile = n_tiles[j]

            def one_pass(p, carry, j=j, n_tile=n_tile):
                parts = []
                for g in range(GROUP):
                    t = p * GROUP + g
                    live = t < n_tile
                    e = jnp.where(live, tile_e[j * TILES + t], 0)
                    at = jnp.where(live, tile_row[j * TILES + t], 0)
                    base = jnp.where(live, tile_rank[j * TILES + t], -1000)
                    kb[g * TILE:(g + 1) * TILE, :] = obuf[pl.ds(pl.multiple_of(at, TILE), TILE), :]
                    rows = lax.broadcasted_iota(I32, (TILE, LANES), 0) + base
                    hit = rows.astype(F32) == rank[j, pl.ds(e, 1), :]
                    parts.append(jnp.where(hit, wrow[j, pl.ds(e, 1), :], ZERO))
                st = jnp.transpose(jnp.concatenate(parts, axis=0))
                res = dot(jnp.concatenate(split3(st), axis=0), kb[...])
                res = res[:LANES] + res[LANES:256] + res[256:]
                fresh = (first == 0) & (p == 0)

                @pl.when(fresh)
                def _():
                    pv[j * LANES:(j + 1) * LANES, :] = res

                @pl.when(jnp.logical_not(fresh))
                def _():
                    pv[j * LANES:(j + 1) * LANES, :] += res
                return carry

            @pl.when((first == 0) & (n_tile == 0))
            def _():
                pv[j * LANES:(j + 1) * LANES, :] = jnp.zeros((LANES, pv.shape[1]), F32)
            lax.fori_loop(0, (n_tile + GROUP - 1) >> CHIPS, one_pass, 0)

            @pl.when(last)
            def _():
                finish(j)

    def wait_for(k, carry):
        for cp in fetch(k):
            cp.wait()
        return carry

    def batch(bt, nxt):
        first = bt * MAXENT
        n_ent = jnp.minimum(n_all - first, MAXENT)

        def collect(q, carry):
            es = [jnp.minimum(q * TAKE + g, n_ent - 1) + first for g in range(TAKE)]
            ext = functools.reduce(jnp.logical_or, [starts[ent_e[n], n_blk] > starts[ent_e[n], PEERS] for n in es])

            def take(width):
                sel = []
                for n in es:
                    rows = (lax.broadcasted_iota(I32, (UNIT, LANES), 0) + ent_u[n] * UNIT).astype(F32)
                    e = ent_e[n]
                    sel.append(jnp.concatenate([jnp.where(rows == rank[j, pl.ds(e, 1), :], ONE, ZERO).astype(BF16)
                                                for j in range(width // LANES)], axis=1))
                got = dot(jnp.concatenate(sel, axis=0), xv[:width, :])
                obuf[pl.ds(pl.multiple_of(q * TAKE * UNIT, UNIT), TAKE * UNIT), :] = got.astype(BF16)

            @pl.when(ext)
            def _():
                take(n_tok)

            @pl.when(jnp.logical_not(ext))
            def _():
                take(n_main)
            return carry

        lax.fori_loop(0, (n_ent + TAKE - 1) // TAKE, collect, 0)

        def run_ffn(k, nxt):
            i = ent_i[first + k]

            def settle(k, carry):
                wait_for(k, carry)

                @pl.when(k < i)
                def _():
                    start(k + NBUF)
                return carry
            lax.fori_loop(nxt, i + 1, settle, 0)
            b = lax.rem(i, NBUF)
            two = (k + 1 < n_ent) & (ent_i[first + k + 1] == i)

            def ffn(n):
                rows = pl.ds(pl.multiple_of(k * UNIT, UNIT), n)
                xg = obuf[rows, :]
                act = (jax.nn.silu(dot(xg, b1[b])) * dot(xg, b3[b])).astype(BF16)
                obuf[rows, :] = dot(act, b2[b]).astype(BF16)

            @pl.when(two)
            def _():
                ffn(2 * UNIT)

            @pl.when(jnp.logical_not(two))
            def _():
                ffn(UNIT)
            end = k + jnp.where(two, 2, 1)

            @pl.when((first + end == n_all) | (ent_i[first + end] != i))
            def _():
                start(i + NBUF)
            return end, jnp.maximum(nxt, i + 1)

        nxt = lax.while_loop(lambda s: s[0] < n_ent, lambda s: run_ffn(*s), (0, nxt))[1]
        flush(first, n_ent, first + n_ent == n_all)
        return nxt

    nxt = lax.fori_loop(0, (n_all + MAXENT - 1) // MAXENT, batch, 0)

    def drain(k, carry):
        wait_for(k, carry)
        start(k + NBUF)
        return carry

    lax.fori_loop(nxt, n_act, drain, 0)

    @pl.when(n_all == 0)
    def _():
        pv[...] = jnp.zeros_like(pv)
        for j in range(n_blk):
            finish(j)
    for j in range(n_blk):
        out_copies(j).wait()


def scatter_kernel(pm_hbm, pe_hbm, z_ref, gw_ref, y_ref,
                   out_ref, mo, md, mrg, mrf, mrs, mfin, eo, ed, erg, erf, ers, gsib, ecr, ssem, rsem, lsem):
    me, c, h, sib, yn, zn, mir, first, second, diag = dims()
    cols = mo.shape[-1]
    mine = pl.ds(pl.multiple_of(c * cols, LANES), cols)
    theirs = pl.ds(pl.multiple_of((1 - c) * cols, LANES), cols)
    local, peer = [], []
    for base, (src, own, got, chips, swap) in ((0, (pe_hbm, eo, ed, (diag, yn, zn, me), (0, 1, 2, 3))),
                                               (CHIPS, (pm_hbm, mo, md, (diag, first, second, me), (0, 2, 1, 3)))):
        for i in range(CHIPS):
            rows = pl.ds(2 * ((chips[i] % PEERS) // 2), 2)
            sib_rows = pl.ds(2 * ((chips[swap[i]] % PEERS) // 2), 2)
            local.append(pltpu.make_async_copy(src.at[rows, :, mine], own.at[i], lsem.at[base + i]))
            peer.append(pltpu.make_async_remote_copy(
                src_ref=src.at[sib_rows, :, theirs], dst_ref=got.at[i], send_sem=ssem.at[base + i],
                recv_sem=rsem.at[base + i], device_id={"ep": sib}, device_id_type=MESH))
    for i in (0, CHIPS, 1, 5, 2, 6, 3, 7):
        local[i].start()
    barrier([{"ep": sib}, {"ep": yn}, {"ep": zn}, {"ep": mir}])
    for i in (0, CHIPS, 1, 5, 2, 6, 3, 7):
        peer[i].start()

    def rcopy(src, dst, i, dev):
        return pltpu.make_async_remote_copy(src_ref=src, dst_ref=dst, send_sem=ssem.at[i], recv_sem=rsem.at[i],
                                            device_id={"ep": dev}, device_id_type=MESH)

    eg, ef, es = rcopy(eo.at[0], erg, PEERS, yn), rcopy(eo.at[1], erf, 9, yn), rcopy(eo.at[2], ers, 10, zn)
    back = rcopy(eo.at[3], ecr, 11, mir)
    gshare = rcopy(gw_ref, gsib, 12, sib)
    order = (1 - c, c)
    mg = [rcopy(mo.at[0, b], mrg.at[b], 13 + n, first) for n, b in enumerate(order)]
    ms = [rcopy(mo.at[2, b], mrs.at[b], 15 + n, second) for n, b in enumerate(order)]
    mf = rcopy(mo.at[1], mrf, 17, first)
    mfinal = rcopy(mo.at[3, 1 - c], mfin, 18, sib)

    def joined(own, got, i, base):
        local[base + i].wait()
        peer[base + i].wait_recv()
        own[i] = own[i] + got[i]

    joined(eo, ed, 0, 0)
    eg.start()
    joined(mo, md, 0, CHIPS)
    mg[0].start()
    joined(eo, ed, 1, 0)
    ef.start()
    mg[1].start()
    joined(eo, ed, 2, 0)
    joined(eo, ed, 3, 0)
    gshare.start()
    eg.wait_recv()
    eo[2] = eo[2] + erg[...]
    es.start()
    joined(mo, md, 1, CHIPS)
    mf.start()
    joined(mo, md, 2, CHIPS)
    mg[0].wait_recv()
    mo[2, 1 - c] = mo[2, 1 - c] + mrg[1 - c]
    ms[0].start()
    ef.wait_recv()
    es.wait_recv()
    eo[3] = eo[3] + erf[...] + ers[...]
    back.start()
    joined(mo, md, 3, CHIPS)
    out_ref[...] = z_ref[...]
    mg[1].wait_recv()
    mo[2, c] = mo[2, c] + mrg[c]
    ms[1].start()
    mf.wait_recv()
    mo[3] = mo[3] + mrf[...]
    gshare.wait_recv()
    back.wait_recv()
    for b, g in ((c, gw_ref), (1 - c, gsib)):
        for part in split3(g[...]):
            mo[3, b] += dot(part, ecr[b], 0, 0)
    ms[0].wait_recv()
    mo[3, 1 - c] = mo[3, 1 - c] + mrs[1 - c]
    mfinal.start()
    ms[1].wait_recv()
    out_ref[:, mine] += mo[3, c] + mrs[c]
    mfinal.wait_recv()
    out_ref[:, theirs] += mfin[...]
    y_ref[...] = out_ref[...].astype(y_ref.dtype)
    for cp in peer + mg + ms + [eg, ef, es, back, gshare, mf, mfinal]:
        cp.wait_send()


def solution(mesh):
    any_space = pl.BlockSpec(memory_space=pl.ANY)
    vmem = pl.BlockSpec(memory_space=pltpu.VMEM)
    smem = pl.BlockSpec(memory_space=pltpu.SMEM)
    sds = jax.ShapeDtypeStruct

    def gather(x, at, se, rnd, wr, w1, w3, w2):
        d, ff = w1.shape
        return pl.pallas_call(
            gather_kernel,
            out_shape=(sds((PEERS, LANES, d), BF16), sds((PEERS, EXT, d), BF16), sds((PEERS, 16, LANES), F32),
                       sds((PEERS, PEERS, LANES), F32), sds((PEERS, LANES), I32), sds((EXT, LANES), F32),
                       sds((LANES, d), F32), sds((1, 1), I32)),
            in_specs=[vmem, vmem, vmem, smem, vmem] + [any_space] * 3,
            out_specs=(any_space,) * CHIPS + (vmem,) * CHIPS,
            scratch_shapes=[
                pltpu.VMEM((PEERS, LANES, d), BF16), pltpu.VMEM((PEERS, EXT, d), BF16),
                pltpu.VMEM((PEERS, 16, LANES), F32), pltpu.VMEM((PEERS, PEERS, LANES), F32),
                pltpu.VMEM((EXT, d), BF16), pltpu.VMEM((PEERS, LANES), F32),
                pltpu.VMEM((EXT, d), BF16), pltpu.VMEM((PEERS, LANES), F32), pltpu.VMEM((16, LANES), F32),
                pltpu.VMEM((2, NUM_EXPERTS, LANES), F32), pltpu.VMEM((NUM_EXPERTS, LANES), F32),
                pltpu.VMEM((5, PEERS, LANES), F32), pltpu.VMEM((5, PEERS, LANES), F32),
                pltpu.VMEM((d, ff), BF16), pltpu.VMEM((d, ff), BF16), pltpu.VMEM((ff, d), BF16),
                pltpu.SemaphoreType.DMA((60,)), pltpu.SemaphoreType.DMA((60,)), pltpu.SemaphoreType.DMA((21,)),
            ],
            compiler_params=pltpu.CompilerParams(collective_id=0, has_side_effects=True),
            name="gather_rows",
        )(x, at, se, rnd, wr, w1, w3, w2)

    def experts(own, se, xm, xe, wm, we, w1, w3, w2):
        _, d, ff = w1.shape
        n_tok = PEERS * (LANES + EXT)
        return pl.pallas_call(
            expert_kernel,
            out_shape=(sds((PEERS * LANES, d), F32), sds((PEERS * EXT, d), BF16)),
            in_specs=[smem, smem, any_space, any_space, vmem, vmem] + [any_space] * 3,
            out_specs=(any_space, any_space),
            scratch_shapes=[
                pltpu.VMEM((n_tok, d), BF16), pltpu.VMEM((n_tok // LANES, NUM_EXPERTS, LANES), F32), pltpu.VMEM((n_tok // LANES, NUM_EXPERTS, LANES), F32),
                pltpu.VMEM((n_tok, d), F32), pltpu.VMEM((PEERS * EXT, d), BF16), pltpu.VMEM((MAXENT * UNIT, d), BF16),
                pltpu.VMEM((GROUP * TILE, d), BF16),
                pltpu.VMEM((NUM_EXPERTS, LANES), I32), pltpu.SMEM((NUM_EXPERTS, LANES), I32),
                pltpu.VMEM((NBUF, d, ff), BF16), pltpu.VMEM((NBUF, d, ff), BF16), pltpu.VMEM((NBUF, ff, d), BF16),
                pltpu.SMEM((32,), I32), pltpu.SMEM((32,), I32), pltpu.SMEM((NUM_EXPERTS,), I32),
                pltpu.SMEM((384,), I32), pltpu.SMEM((384,), I32), pltpu.SMEM((384,), I32),
                pltpu.SMEM((12 * TILES,), I32), pltpu.SMEM((12 * TILES,), I32), pltpu.SMEM((12 * TILES,), I32),
                pltpu.SMEM((16,), I32),
                pltpu.SemaphoreType.DMA((3, NBUF)), pltpu.SemaphoreType.DMA((3,)), pltpu.SemaphoreType.DMA((12,)),
            ],
            name="expert_rows",
        )(own, se, xm, xe, wm, we, w1, w3, w2)

    def scatter(pm, pe, z, gw, last):
        d = z.shape[1]
        half = d // 2
        big, small = (2, LANES, half), (2, EXT, half)
        return pl.pallas_call(
            scatter_kernel,
            out_shape=sds((LANES, d), F32),
            in_specs=[any_space, any_space, vmem, vmem],
            out_specs=vmem,
            scratch_shapes=[
                pltpu.VMEM((LANES, d), F32),
                pltpu.VMEM((CHIPS,) + big, F32), pltpu.VMEM((CHIPS,) + big, F32),
                pltpu.VMEM(big, F32), pltpu.VMEM(big, F32), pltpu.VMEM(big, F32), pltpu.VMEM((LANES, half), F32),
                pltpu.VMEM((CHIPS,) + small, BF16), pltpu.VMEM((CHIPS,) + small, BF16),
                pltpu.VMEM(small, BF16), pltpu.VMEM(small, BF16), pltpu.VMEM(small, BF16), pltpu.VMEM((EXT, LANES), F32),
                pltpu.VMEM(small, BF16),
                pltpu.SemaphoreType.DMA((20,)), pltpu.SemaphoreType.DMA((20,)), pltpu.SemaphoreType.DMA((PEERS,)),
            ],
            compiler_params=pltpu.CompilerParams(collective_id=1 if last else 2, has_side_effects=True),
            name="scatter_sums" if last else "scatter_more",
        )(pm, pe, z, gw)

    def device_step(x, slot_expert, w1, w3, w2, assign, wr, w1s, w3s, w2s):
        d = x.shape[1]
        rows_of = lambda a: a.reshape(-1, d)

        def gathered(r):
            return gather(x, assign.T, slot_expert, r.reshape(1), wr.T, w1s, w3s, w2s)

        def summed(parts):
            xm, xe, wm, we, own = parts
            pm, pe = experts(own, slot_expert, rows_of(xm), rows_of(xe), wm, we, w1, w3, w2)
            return pm.reshape(PEERS, LANES, d), pe.reshape(PEERS, EXT, d)

        def again(carry):
            r, n, z = carry
            *parts, gw, _, _ = gathered(r)
            return r + 1, n, scatter(*summed(parts), z, gw, False)

        *parts, gw, z, nr = gathered(jnp.int32(0))
        z = lax.while_loop(lambda s: s[0] < s[1], again, (jnp.int32(1), nr.reshape(()), z))[2]
        return scatter(*summed(parts), z, gw, True).astype(BF16)

    tok = P(("dp", "ep"), None)
    slot = P("ep", None, None)
    return jax.shard_map(device_step, mesh=mesh,
                         in_specs=(tok, P(), slot, slot, slot, tok, P(), P(), P(), P()),
                         out_specs=tok, check_vma=False)
```

time: 112 us -> 112 us (level)
  Pallas kernels: 110 us -> 108 us
where the time goes in v3:
time: 112 us; the launch traced here: 111 us
  Pallas kernels  108 us (96%)
  other arithmetic  1.92 us (2%)
    pallas_call x1, Pallas kernels, scatter(): pl.pallas_call(scatter_kernel, out_shape=sds((LANES, d), F32), in_specs=[...  43.1 us
    pallas_call x1, Pallas kernels, gather(): pl.pallas_call(gather_kernel, out_shape=(sds((PEERS, LANES, d), BF16), sd...  39.2 us
    pallas_call x1, Pallas kernels, experts(): pl.pallas_call(expert_kernel, out_shape=(sds((PEERS * LANES, d), F32), sd...  26.2 us

profile of v3, /device:TPU:0, one launch (start us, length us, event | category | flops | bytes accessed | tf_op | source)
XLA Modules:
  0.0 111.3 jit_solution(9881830105695530227)
XLA Ops:
  0.0 0.0 copy-start
  0.0 0.0 copy-start.2
  0.0 0.0 copy-start.3
  0.0 0.0 copy-start.4
  0.0 39.2 %gather_rows.2 = (bf16[8,128,1536]{2,1,0:T(8,128)(2,1)}, bf16[8,64,1536]{2,1,0:T(8,128)(2,1)}, f32[8,16,128]{2,1,0:T(8,128)}, f32[8,8,128]{2,1,0:T(8,128)}, s32[...) custom-call(bf16[128,1536]{1,0:T(8,128)(2,1)} %x_ref.1, s32[6,128]{1,0:T(8,128)} %bitcast.38, ...), custom_call_target="tpu_custom_call" | custom-call | tf_op jit(solution)/shard_map/gather_rows/pallas_call | solution.py:624
  39.2 0.0 copy-done
  39.2 0.0 copy-done.2
  39.2 0.0 copy-done.3
  39.2 0.0 copy-done.4
  39.3 0.8 while.10
  40.1 0.0 copy-start.1
  40.1 26.2 %expert_rows.2 = (f32[1024,1536]{1,0:T(8,128)}, bf16[512,1536]{1,0:T(8,128)(2,1)}) custom-call(s32[8,128]{1,0:T(8,128)} %get-tuple-element.91.own_ref, s32[320]{0:T(512)S(1)} %get-tuple-element.269, bf16[1024,1536]{1,0:T(8,128)(2,1)} %bitcast.35, bf16[512,1536]{1,0:T(8,128)(2,1)} %bitcast.37, f32[8,16,128]{2,1,0:T(8,128)} %get-tuple-element.94.wm_ref, ...), custom_call_target="tpu_custom_call" | custom-call | tf_op jit(solution)/shard_map/expert_rows/pallas_call | solution.py:648
  66.3 0.0 copy-done.1
  66.3 43.1 %scatter_sums.1 = f32[128,1536]{1,0:T(8,128)} custom-call(f32[8,128,1536]{2,1,0:T(8,128)} %bitcast.34, bf16[8,64,1536]{2,1,0:T(8,128)(2,1)} %bitcast.36, f32[128,1536]{1,0:T(8,128)S(1)} %copy-done.1, f32[64,128]{1,0:T(8,128)} %get-tuple-element.101.gw_ref), custom_call_target="tpu_custom_call" | custom-call | tf_op jit(solution)/shard_map/scatter_sums/pallas_call | solution.py:672
  109.4 1.9 %convert_element_type.3 = bf16[128,1536]{1,0:T(8,128)(2,1)} convert(f32[128,1536]{1,0:T(8,128)} %scatter_sums.1) | non-fusion elementwise | flops 196608 | bytes 1179648 | tf_op jit(solution)/shard_map/convert_element_type | solution.py:709
Async XLA Ops:
  0.0 39.2 %copy-start = (bf16[1536,1024]{1,0:T(8,128)(2,1)S(1)}, bf16[1536,1024]{1,0:T(8,128)(2,1)}, u32[]{:S(2)}) copy-start(bf16[1536,1024]{1,0:T(8,128)(2,1)} %w1_hbm.2) | copy-start | bytes 9437188
  0.0 39.2 %copy-start.2 = (bf16[128,1536]{1,0:T(8,128)(2,1)S(1)}, bf16[128,1536]{1,0:T(8,128)(2,1)}, u32[]{:S(2)}) copy-start(bf16[128,1536]{1,0:T(8,128)(2,1)} %x_ref.1) | copy-start | bytes 1179652
  0.0 39.2 %copy-start.3 = (s32[320]{0:T(512)S(1)}, s32[320]{0:T(512)}, u32[]{:S(2)}) copy-start(s32[320]{0:T(512)} %se_ref.3) | copy-start | bytes 3844
  0.0 39.2 %copy-start.4 = (s32[128,6]{0,1:T(8,128)S(1)}, s32[128,6]{0,1:T(8,128)}, u32[]{:S(2)}) copy-start(s32[128,6]{0,1:T(8,128)} %param.17) | copy-start | bytes 9220
  40.1 26.2 %copy-start.1 = (f32[128,1536]{1,0:T(8,128)S(1)}, f32[128,1536]{1,0:T(8,128)}, u32[]{:S(2)}) copy-start(f32[128,1536]{1,0:T(8,128)} %get-tuple-element.100.z_ref) | copy-start | bytes 2359300

commit v4 on v3

--- a/solution.py
+++ b/solution.py
@@ -18,6 +18,7 @@
 NBUF = 6
 MAXENT = 15
 GROUP = 16
+FEW = 4
 TILES = 160
 TILE_BITS = CHIPS
 TILE = 1 << TILE_BITS
@@ -178,7 +179,7 @@
     lane = lax.broadcasted_iota(I32, (1, LANES), 1).astype(F32)
     block_key = jnp.where(cand > ZERO, jnp.broadcast_to(lane, cand.shape), 1e9)
     cand_s[0] = block_key
-    there = jnp.where(jnp.sum(eye * (ONE - here), axis=1, keepdims=True) > ZERO, ONE, 2.0)
+    there = jnp.where(jnp.sum(eye * (ONE - here), axis=1, keepdims=True) > ZERO, 2.0, 5.0)
     cand_s[1] = jnp.broadcast_to(several * there, cand.shape)
     load0 = jnp.sum(cand * (ONE - several) * there, axis=0, keepdims=True)
 
@@ -401,10 +402,12 @@
         for j in range(n_blk):
             n_tile = n_tiles[j]
 
-            def one_pass(p, carry, j=j, n_tile=n_tile):
+            joint = GROUP if j < PEERS else FEW
+
+            def one_pass(p, carry, j=j, n_tile=n_tile, joint=joint):
                 parts = []
-                for g in range(GROUP):
-                    t = p * GROUP + g
+                for g in range(joint):
+                    t = p * joint + g
                     live = t < n_tile
                     e = jnp.where(live, tile_e[j * TILES + t], 0)
                     at = jnp.where(live, tile_row[j * TILES + t], 0)
@@ -414,7 +417,7 @@
                     hit = rows.astype(F32) == rank[j, pl.ds(e, 1), :]
                     parts.append(jnp.where(hit, wrow[j, pl.ds(e, 1), :], ZERO))
                 st = jnp.transpose(jnp.concatenate(parts, axis=0))
-                res = dot(jnp.concatenate(split3(st), axis=0), kb[...])
+                res = dot(jnp.concatenate(split3(st), axis=0), kb[:joint * TILE, :])
                 res = res[:LANES] + res[LANES:256] + res[256:]
                 fresh = (first == 0) & (p == 0)
 
@@ -430,7 +433,7 @@
             @pl.when((first == 0) & (n_tile == 0))
             def _():
                 pv[j * LANES:(j + 1) * LANES, :] = jnp.zeros((LANES, pv.shape[1]), F32)
-            lax.fori_loop(0, (n_tile + GROUP - 1) >> CHIPS, one_pass, 0)
+            lax.fori_loop(0, (n_tile + joint - 1) // joint, one_pass, 0)
 
             @pl.when(last)
             def _():
@@ -671,7 +674,7 @@
         big, small = (2, LANES, half), (2, EXT, half)
         return pl.pallas_call(
             scatter_kernel,
-            out_shape=sds((LANES, d), F32),
+            out_shape=sds((LANES, d), BF16 if last else F32),
             in_specs=[any_space, any_space, vmem, vmem],
             out_specs=vmem,
             scratch_shapes=[
@@ -706,7 +709,7 @@
 
         *parts, gw, z, nr = gathered(jnp.int32(0))
         z = lax.while_loop(lambda s: s[0] < s[1], again, (jnp.int32(1), nr.reshape(()), z))[2]
-        return scatter(*summed(parts), z, gw, True).astype(BF16)
+        return scatter(*summed(parts), z, gw, True)
 
     tok = P(("dp", "ep"), None)
     slot = P("ep", None, None)

time: 112 us -> 111 us (level)
  other arithmetic: 1.92 us -> 0 us
  local copies, waits for them, and re-layouts: 0.02 us -> 1.79 us
    convert_element_type x1 -> x0, other arithmetic: 1.92 us -> none  [device_step(): return scatter(*summed(parts), z, gw, True).astype(BF16)]
    pallas_call x1, Pallas kernels: 26.2 us -> 24.4 us  [experts(): pl.pallas_call(expert_kernel, out_shape=(sds((PEERS * LANES, d), F32), sd...]
    unnamed x10 -> x11, local copies, waits for them, and re-layouts: 0.02 us -> 1.79 us
where the time goes in v4:
time: 111 us; the launch traced here: 110 us
  Pallas kernels  107 us (96%)
  local copies, waits for them, and re-layouts  1.79 us (2%)
    pallas_call x1, Pallas kernels, scatter(): pl.pallas_call(scatter_kernel, out_shape=sds((LANES, d), BF16 if last els...  43.3 us
    pallas_call x1, Pallas kernels, gather(): pl.pallas_call(gather_kernel, out_shape=(sds((PEERS, LANES, d), BF16), sd...  39.2 us
    pallas_call x1, Pallas kernels, experts(): pl.pallas_call(expert_kernel, out_shape=(sds((PEERS * LANES, d), F32), sd...  24.4 us

profile of v4, /device:TPU:0, one launch (start us, length us, event | category | flops | bytes accessed | tf_op | source)
XLA Modules:
  0.0 109.6 jit_solution(10782482250076312433)
XLA Ops:
  0.0 0.0 copy-start
  0.0 0.0 copy-start.2
  0.0 0.0 copy-start.3
  0.0 0.0 copy-start.4
  0.0 39.2 %gather_rows.2 = (bf16[8,128,1536]{2,1,0:T(8,128)(2,1)}, bf16[8,64,1536]{2,1,0:T(8,128)(2,1)}, f32[8,16,128]{2,1,0:T(8,128)}, f32[8,8,128]{2,1,0:T(8,128)}, s32[...) custom-call(bf16[128,1536]{1,0:T(8,128)(2,1)} %x_ref.1, s32[6,128]{1,0:T(8,128)} %bitcast.38, ...), custom_call_target="tpu_custom_call" | custom-call | tf_op jit(solution)/shard_map/gather_rows/pallas_call | solution.py:627
  39.2 0.0 copy-done
  39.2 0.0 copy-done.2
  39.2 0.0 copy-done.3
  39.2 0.0 copy-done.4
  39.3 0.8 while.10
  40.1 0.0 copy-start.1
  40.1 24.4 %expert_rows.2 = (f32[1024,1536]{1,0:T(8,128)}, bf16[512,1536]{1,0:T(8,128)(2,1)}) custom-call(s32[8,128]{1,0:T(8,128)} %get-tuple-element.91.own_ref, s32[320]{0:T(512)S(1)} %get-tuple-element.269, bf16[1024,1536]{1,0:T(8,128)(2,1)} %bitcast.35, bf16[512,1536]{1,0:T(8,128)(2,1)} %bitcast.37, f32[8,16,128]{2,1,0:T(8,128)} %get-tuple-element.94.wm_ref, ...), custom_call_target="tpu_custom_call" | custom-call | tf_op jit(solution)/shard_map/expert_rows/pallas_call | solution.py:651
  64.5 0.0 copy-done.1
  64.5 43.3 %scatter_sums.1 = bf16[128,1536]{1,0:T(8,128)(2,1)} custom-call(f32[8,128,1536]{2,1,0:T(8,128)} %bitcast.34, bf16[8,64,1536]{2,1,0:T(8,128)(2,1)} %bitcast.36, f32[128,1536]{1,0:T(8,128)S(1)} %copy-done.1, f32[64,128]{1,0:T(8,128)} %get-tuple-element.101.gw_ref), custom_call_target="tpu_custom_call" | custom-call | tf_op jit(solution)/shard_map/scatter_sums/pallas_call | solution.py:675
  107.8 1.8 %copy.20 = bf16[128,1536]{1,0:T(8,128)(2,1)} copy(bf16[128,1536]{1,0:T(8,128)(2,1)} %scatter_sums.1) | data formatting | bytes 786432
Async XLA Ops:
  0.0 39.2 %copy-start = (bf16[1536,1024]{1,0:T(8,128)(2,1)S(1)}, bf16[1536,1024]{1,0:T(8,128)(2,1)}, u32[]{:S(2)}) copy-start(bf16[1536,1024]{1,0:T(8,128)(2,1)} %w1_hbm.2) | copy-start | bytes 9437188
  0.0 39.2 %copy-start.2 = (bf16[128,1536]{1,0:T(8,128)(2,1)S(1)}, bf16[128,1536]{1,0:T(8,128)(2,1)}, u32[]{:S(2)}) copy-start(bf16[128,1536]{1,0:T(8,128)(2,1)} %x_ref.1) | copy-start | bytes 1179652
  0.0 39.2 %copy-start.3 = (s32[320]{0:T(512)S(1)}, s32[320]{0:T(512)}, u32[]{:S(2)}) copy-start(s32[320]{0:T(512)} %se_ref.3) | copy-start | bytes 3844
  0.0 39.2 %copy-start.4 = (s32[128,6]{0,1:T(8,128)S(1)}, s32[128,6]{0,1:T(8,128)}, u32[]{:S(2)}) copy-start(s32[128,6]{0,1:T(8,128)} %param.17) | copy-start | bytes 9220
  40.1 24.4 %copy-start.1 = (f32[128,1536]{1,0:T(8,128)S(1)}, f32[128,1536]{1,0:T(8,128)}, u32[]{:S(2)}) copy-start(f32[128,1536]{1,0:T(8,128)} %get-tuple-element.100.z_ref) | copy-start | bytes 2359300
